TPU v7x, 32 devices: a whole 2x2x4 slice. The times are simulated.
32 devices in a mesh: blk: 4 (over y, core), grp: 8 (over z, x).
Axes of the slice: x: 2, y: 2, z: 4, core: 2. Of those that a mesh axis runs over, the one named last changes fastest.
Arguments:
- gas_state: bfloat16 [16, 32, 32768], P(None, None, ('grp', 'blk')), may hold values from -6 to 6
- cos_zenith: bfloat16 [32768], P(('grp', 'blk')), may hold values from 0.049804688 to 1
- daylit: int32 [32768], P(('grp', 'blk')), may hold values from 0 to 1
- fine_area: float32 [131072], P(('grp', 'blk')), may hold values from 0.25 to 4
- fine_albedo: float32 [2, 131072], P(None, ('grp', 'blk')), may hold values from 0.05 to 0.85
- parent_of: int32 [131072], P(('grp', 'blk')), may hold values from 0 to 4095, as said below
- optics_weight: bfloat16 [64, 16], replicated, may hold values from -1.5 to 1.5
- solar_weight: float32 [32], replicated, may hold values from 0.01 to 0.1
- neighbours: int32 [3, 32768], P(None, ('grp', 'blk')), may hold values from 0 to 32767, as said below
- side_weight: float32 [3, 32768], P(None, ('grp', 'blk')), may hold values from 0.05 to 0.3
Outputs:
- fluxes: float32 [2, 33, 32768], P(None, None, ('grp', 'blk'))
Inputs may be any that keep to these rules, and one draw needn't show every extreme that they name: `parent_of`: the fine cells of one index of grp have their parents among that index's columns, numbered from 0 within it; each column has exactly 4 fine cells, and the 128 fine cells of an aligned block share 128 // 4 consecutive columns. `neighbours`: every neighbour lies within 128 columns of its column and among the columns of the same index of grp; a neighbour may be the column itself.
All inputs are finite; a program needn't handle non-finite values.
Results may differ from a plain program's by a relative error of at most 0.0003.
Values may be sent and summed in bfloat16 or wider, within the bound.
A program may use at most 64 MiB of HBM per device.

v0:
```python
import functools
import math

import jax
import jax.numpy as jnp
from jax import lax
from jax.experimental import pallas as pl
from jax.experimental.pallas import tpu as pltpu
from jax.sharding import PartitionSpec as P

CB = 128
FB = 128
ASYM = 0.8
TAU_SCALE = 0.08
SSA_MAX = 0.98
LOG2E = math.log2(math.e)
CHUNK = 8
VMEM = pltpu.VMEM


def round_up(value, multiple):
    return -(-value // multiple) * multiple


def local_albedo(area_ref, albedo_ref, parent_ref, span):
    blocks = area_ref.shape[0]
    area = area_ref[...]
    rows = [
        jnp.concatenate([albedo_ref[s : s + 1, b * FB : (b + 1) * FB] for b in range(blocks)], axis=0)
        for s in range(2)
    ]
    weights = jnp.transpose(jnp.concatenate([area, area * rows[0], area * rows[1]], axis=0))
    parent = jnp.transpose(jnp.concatenate([parent_ref[...]] * 3, axis=0))
    inside = parent & (span - 1)
    totals = jnp.concatenate(
        [jnp.sum(jnp.where(inside == j, weights, 0.0), axis=0, keepdims=True) for j in range(span)], axis=0
    )
    share = totals[:, :blocks]
    first = (totals[:, blocks : 2 * blocks] / share).astype(jnp.bfloat16).astype(jnp.float32)
    second = (totals[:, 2 * blocks :] / share).astype(jnp.bfloat16).astype(jnp.float32)
    number = (parent[0:1, :blocks] // span).astype(jnp.float32)
    return first, second, number


def pick_albedo(pieces, start_span, span, blocks, ncb):
    per = CB // span
    table = jnp.concatenate(
        [jnp.concatenate([p[0:span, s * blocks : (s + 1) * blocks] for p in pieces], axis=1) for s in range(2)],
        axis=0,
    ).astype(jnp.bfloat16)
    number = jnp.concatenate([p[span : span + 1, 0:blocks] for p in pieces], axis=1).astype(jnp.int32)
    total = number.shape[1]
    row = lax.broadcasted_iota(jnp.int32, (ncb, total), 0) * per + start_span
    parts = []
    for m in range(per):
        chosen = (number == row + m).astype(jnp.float32).astype(jnp.bfloat16)
        parts.append(
            lax.dot_general(chosen, table, (((1,), (1,)), ((), ())), preferred_element_type=jnp.float32)
        )
    direct = jnp.concatenate([p[:, 0:span] for p in parts], axis=1)
    diffuse = jnp.concatenate([p[:, span : 2 * span] for p in parts], axis=1)
    return direct, diffuse


def expand_weight(weight_ref, big_ref):
    feats, rows = weight_ref.shape
    half = big_ref.shape[1] // feats
    wide = feats * half
    source = lax.broadcasted_iota(jnp.int32, (feats, wide), 0)
    column = lax.broadcasted_iota(jnp.int32, (feats, wide), 1)
    spread = (column // half == source).astype(jnp.float32).astype(jnp.bfloat16)
    repeated = lax.dot_general(
        weight_ref[...], spread, (((0,), (0,)), ((), ())), preferred_element_type=jnp.float32
    )
    row = lax.broadcasted_iota(jnp.int32, (rows, wide), 0)
    repeated = jnp.where(row < rows // 2, repeated, 0.5 * repeated)
    level = lax.broadcasted_iota(jnp.int32, (rows, wide), 1) % half
    for l in range(half):
        big_ref[l * rows : (l + 1) * rows, :] = jnp.where(level == l, repeated, 0.0).astype(jnp.bfloat16)


def layer(mix, gpoints, rate, back, carry):
    direct, big_b, big_q = carry
    x = mix[:gpoints]
    soft = jnp.maximum(x, 0.0) + jnp.log(1.0 + jnp.exp2(jnp.abs(x) * (-LOG2E)))
    below = direct * jnp.exp2(soft * rate)
    swing = (0.5 * SSA_MAX) * jnp.tanh(mix[gpoints:])
    w = swing + 0.5 * SSA_MAX
    absorbed = (1.0 - 0.5 * SSA_MAX) - swing
    g2 = (0.375 * (1.0 - ASYM)) * w
    g1 = absorbed + g2
    square = absorbed * (g1 + g2)
    k = square * lax.rsqrt(square)
    q = jnp.exp2((k * soft) * (-2.0 * TAU_SCALE * LOG2E))
    q2 = q * q
    kp = k + g1
    km = k - g1
    d = kp + km * q2
    dd = km + kp * q2
    r = g2 - g2 * q2
    t2 = (k + k) * q
    scattered = w * (direct - below)
    rising = scattered * back
    falling = scattered - rising
    z = 1.0 / (d - r * big_b)
    t = t2 * z
    s = (r * big_q + d * rising) * z
    new_b = (r + dd * big_b) * z
    new_q = t * (big_q + big_b * rising) + falling
    return t, s, (below, new_b, new_q)


def product(block, part, turn, gas_ref, big_ref, mix_ref):
    feats = gas_ref.shape[0]
    half = big_ref.shape[1] // feats
    rows = mix_ref.shape[1]
    cols = pl.ds(pl.multiple_of(block * CB, CB), CB)
    inputs = gas_ref[:, pl.ds(pl.multiple_of(part * half, half), half), cols].reshape(feats * half, CB)
    weight = big_ref[turn * rows : (turn + 1) * rows, :]
    mix_ref[turn] = jnp.dot(weight, inputs, preferred_element_type=jnp.float32)


def descend(cb, after, gas_ref, big_ref, cos_ref, solar, mix_ref, state_ref, end_ref):
    feats, lev = gas_ref.shape[0], gas_ref.shape[1]
    gpoints = solar.shape[0]
    rows = 2 * gpoints
    half = big_ref.shape[1] // feats
    mu = cos_ref[pl.ds(cb, 1), :]
    rate = jnp.broadcast_to((-TAU_SCALE * LOG2E) / mu, (gpoints, CB))
    back = jnp.broadcast_to(0.5 * (1.0 - ASYM * mu), (gpoints, CB))
    top = solar * mu
    zero = jnp.zeros((gpoints, CB), jnp.float32)
    carry = (top, zero, zero)

    turns = half // CHUNK

    def mixed(block, part, turn):
        product(block, part, turn, gas_ref, big_ref, mix_ref)

    def down(part, carry):
        for turn in range(turns):
            if turn + 1 < turns:
                mixed(cb, part, turn + 1)
            for i in range(CHUNK):
                level = part * half + turn * CHUNK + i
                state_ref[2, level] = carry[1]
                state_ref[3, level] = carry[2] + carry[0]
                mix = mix_ref[turn, i * rows : (i + 1) * rows, :]
                t, s, carry = layer(mix, gpoints, rate, back, carry)
                state_ref[0, level] = t
                state_ref[1, level] = s
            if turn == turns - 2:
                last = part == lev // half - 1
                mixed(jnp.where(last, after, cb), jnp.where(last, 0, part + 1), 0)
        return carry

    carry = lax.fori_loop(0, lev // half, down, carry)
    for i in range(3):
        end_ref[i] = carry[i]


def ascend(cb, albedo_ref, lit_ref, state_ref, end_ref, flux_ref):
    lev = state_ref.shape[1]
    lit = lit_ref[pl.ds(cb, 1), :]
    direct, big_b, big_q = end_ref[0], end_ref[1], end_ref[2]
    direct_albedo = albedo_ref[0, pl.ds(cb, 1), :]
    diffuse_albedo = albedo_ref[1, pl.ds(cb, 1), :]
    up = (diffuse_albedo * big_q + direct_albedo * direct) / (1.0 - diffuse_albedo * big_b)
    last = [
        jnp.sum(big_b * up + big_q + direct, axis=0, keepdims=True) * lit,
        jnp.sum(up, axis=0, keepdims=True) * lit,
        jnp.zeros((flux_ref.shape[0] - 2 * lev - 2, CB), jnp.float32),
    ]
    flux_ref[2 * lev :, :] = jnp.concatenate(last, axis=0)

    def back_up(step, up):
        first = pl.multiple_of(lev - CHUNK - step * CHUNK, CHUNK)
        sums = [None] * (2 * CHUNK)
        for i in reversed(range(CHUNK)):
            up = state_ref[0, first + i] * up + state_ref[1, first + i]
            down = state_ref[2, first + i] * up + state_ref[3, first + i]
            sums[2 * i] = jnp.sum(down, axis=0, keepdims=True)
            sums[2 * i + 1] = jnp.sum(up, axis=0, keepdims=True)
        flux_ref[pl.ds(pl.multiple_of(2 * first, 2 * CHUNK), 2 * CHUNK), :] = jnp.concatenate(sums, axis=0) * lit
        return up

    lax.fori_loop(0, lev // CHUNK, back_up, up)


def solar_column(solar_ref):
    row = solar_ref[...]
    n = row.shape[1]
    diagonal = lax.broadcasted_iota(jnp.int32, (n, n), 0) == lax.broadcasted_iota(jnp.int32, (n, n), 1)
    return jnp.sum(jnp.where(diagonal, row, 0.0), axis=1, keepdims=True)


def flux_kernel(
    n, span, gas_hbm, cos_ref, lit_ref, weight_ref, solar_ref, area_ref, fine_albedo_ref, parent_ref,
    flux_ref, big_ref, state_ref, end_ref, albedo_ref, cosf_ref, litf_ref, mine_ref, pieces_ref,
    edge_ref, halo_ref, mix_ref, gas_ref, send_sem, recv_sem, edge_send, edge_recv, gas_sem,
):
    ncb = cos_ref.shape[0]
    blocks = area_ref.shape[0]
    me = lax.axis_index("blk")
    peers = [lax.rem(me + shift, n) for shift in range(1, n)]
    mesh_id = pl.DeviceIdType.MESH

    load = pltpu.make_async_copy(gas_hbm, gas_ref, gas_sem)
    load.start()
    barrier = pltpu.get_barrier_semaphore()
    for peer in peers:
        pl.semaphore_signal(barrier, inc=1, device_id={"blk": peer}, device_id_type=mesh_id)

    first, second, number = local_albedo(area_ref, fine_albedo_ref, parent_ref, span)
    mine_ref[...] = jnp.zeros_like(mine_ref)
    mine_ref[0:span, 0:blocks] = first
    mine_ref[0:span, blocks : 2 * blocks] = second
    mine_ref[span : span + 1, 0:blocks] = number
    expand_weight(weight_ref, big_ref)
    cosf_ref[...] = cos_ref[...].astype(jnp.float32)
    litf_ref[...] = lit_ref[...].astype(jnp.float32)
    solar = solar_column(solar_ref)

    def order(i):
        return jnp.where(i < 2, i * (ncb - 1), i - 1)

    def down(i, slot):
        after = order(jnp.minimum(i + 1, ncb - 1))
        descend(
            order(i), after, gas_ref, big_ref, cosf_ref, solar, mix_ref, state_ref.at[slot], end_ref.at[slot]
        )

    def up(i, slot, target_ref):
        ascend(order(i), albedo_ref, litf_ref, state_ref.at[slot], end_ref.at[slot], target_ref)

    load.wait()
    product(0, 0, 0, gas_ref, big_ref, mix_ref)

    def early_down(i, unused):
        down(i, i)
        return unused

    lax.fori_loop(0, 1, early_down, 0)
    pl.semaphore_wait(barrier, n - 1)
    sends = []
    for i, peer in enumerate(peers):
        copy = pltpu.make_async_remote_copy(
            src_ref=mine_ref,
            dst_ref=pieces_ref.at[i],
            send_sem=send_sem.at[i],
            recv_sem=recv_sem.at[i],
            device_id={"blk": peer},
            device_id_type=mesh_id,
        )
        copy.start()
        sends.append(copy)

    ahead = state_ref.shape[0]
    lax.fori_loop(1, ahead, early_down, 0)
    for copy in sends:
        copy.wait()
    start_span = me * (ncb * CB // span)
    pieces = [mine_ref[...]] + [pieces_ref[i] for i in range(n - 1)]
    direct, diffuse = pick_albedo(pieces, start_span, span, blocks, ncb)
    albedo_ref[0] = direct
    albedo_ref[1] = diffuse

    def edge_up(i, unused):
        up(i, i, edge_ref.at[i])
        return unused

    lax.fori_loop(0, 2, edge_up, 0)
    sends = []
    for i, peer in ((0, peers[-1]), (1, peers[0])):
        copy = pltpu.make_async_remote_copy(
            src_ref=edge_ref.at[i],
            dst_ref=halo_ref.at[i],
            send_sem=edge_send.at[i],
            recv_sem=edge_recv.at[i],
            device_id={"blk": peer},
            device_id_type=mesh_id,
        )
        copy.start()
        sends.append(copy)
    flux_ref[:, CB : 2 * CB] = edge_ref[0]
    flux_ref[:, ncb * CB : (ncb + 1) * CB] = edge_ref[1]

    def own(i):
        return flux_ref.at[:, pl.ds(pl.multiple_of((order(i) + 1) * CB, CB), CB)]

    def early_up(i, unused):
        up(i, i, own(i))
        return unused

    lax.fori_loop(2, ahead, early_up, 0)

    def one(i, unused):
        down(i, 0)
        up(i, 0, own(i))
        return unused

    lax.fori_loop(ahead, ncb, one, 0)
    for copy in sends:
        copy.wait()
    flux_ref[:, 0:CB] = halo_ref[1]
    flux_ref[:, (ncb + 1) * CB :] = halo_ref[0]


def side_block(window, centre, picked, weights):
    rows = window.shape[0]
    high = window.astype(jnp.bfloat16)
    low = (window - high.astype(jnp.float32)).astype(jnp.bfloat16)
    both = jnp.concatenate([high, low], axis=0)
    place = lax.broadcasted_iota(jnp.int32, (window.shape[1], CB), 0)
    result = centre
    for k in range(3):
        chosen = (place == picked[k : k + 1]).astype(jnp.float32).astype(jnp.bfloat16)
        beside = jnp.dot(both, chosen, preferred_element_type=jnp.float32)
        result = result + weights[k : k + 1] * (beside[:rows] + beside[rows:] - centre)
    return result


def side_kernel(padded_ref, neighbours_ref, weights_ref, out_ref):
    interfaces, parts, cols = out_ref.shape
    ncb = cols // CB
    start = (lax.axis_index("grp") * lax.axis_size("blk") + lax.axis_index("blk")) * cols
    for cb in range(ncb):
        own = slice(cb * CB, (cb + 1) * CB)
        picked = neighbours_ref[:, own] - (start + (cb - 1) * CB)
        result = side_block(
            padded_ref[:, cb * CB : (cb + 3) * CB],
            padded_ref[:, (cb + 1) * CB : (cb + 2) * CB],
            picked,
            weights_ref[:, own],
        )
        out_ref[:, :, own] = result[: parts * interfaces].reshape(interfaces, parts, CB)


def local(
    gas_state, cos_zenith, daylit, fine_area, fine_albedo, parent_of,
    optics_weight, solar_weight, neighbours, side_weight,
):
    n = lax.axis_size("blk")
    feats, lev, cols = gas_state.shape
    gpoints = solar_weight.shape[0]
    ncb = cols // CB
    blocks = fine_area.shape[0] // FB
    span = cols // blocks
    rows = round_up(2 * (lev + 1), 8)
    half = 16
    full = pl.BlockSpec(memory_space=VMEM)
    padded = pl.pallas_call(
        functools.partial(flux_kernel, n, span),
        out_shape=jax.ShapeDtypeStruct((rows, cols + 2 * CB), jnp.float32),
        in_specs=[pl.BlockSpec(memory_space=pl.ANY)] + [full] * 7,
        out_specs=full,
        scratch_shapes=[
            VMEM((half * 2 * gpoints, half * feats), jnp.bfloat16),
            VMEM((4, 4, lev, gpoints, CB), jnp.float32),
            VMEM((4, 3, gpoints, CB), jnp.float32),
            VMEM((2, ncb, CB), jnp.float32),
            VMEM((ncb, CB), jnp.float32),
            VMEM((ncb, CB), jnp.float32),
            VMEM((span + 8, 128), jnp.float32),
            VMEM((n - 1, span + 8, 128), jnp.float32),
            VMEM((2, rows, CB), jnp.float32),
            VMEM((2, rows, CB), jnp.float32),
            VMEM((half // CHUNK, CHUNK * 2 * gpoints, CB), jnp.float32),
            VMEM((feats, lev, cols), gas_state.dtype),
            pltpu.SemaphoreType.DMA((n - 1,)),
            pltpu.SemaphoreType.DMA((n - 1,)),
            pltpu.SemaphoreType.DMA((2,)),
            pltpu.SemaphoreType.DMA((2,)),
            pltpu.SemaphoreType.DMA,
        ],
        compiler_params=pltpu.CompilerParams(collective_id=0, has_side_effects=True),
    )(
        gas_state, cos_zenith.reshape(ncb, CB), daylit.reshape(ncb, CB), optics_weight.T,
        solar_weight.reshape(1, gpoints), fine_area.reshape(blocks, FB), fine_albedo,
        parent_of.reshape(blocks, FB),
    )
    result = pl.pallas_call(
        side_kernel,
        out_shape=jax.ShapeDtypeStruct((lev + 1, 2, cols), jnp.float32),
        in_specs=[full] * 3,
        out_specs=full,
    )(padded, neighbours, side_weight)
    return jnp.transpose(result, (1, 0, 2))


def solution(mesh):
    columns = P(("grp", "blk"))
    last = P(None, ("grp", "blk"))
    in_specs = (
        P(None, None, ("grp", "blk")), columns, columns, columns, last, columns, P(), P(), last, last,
    )
    out_specs = P(None, None, ("grp", "blk"))
    return jax.shard_map(local, mesh=mesh, in_specs=in_specs, out_specs=out_specs, check_vma=False)
```

profile of v0, /device:TPU:0, one launch (start us, length us, event | category | flops | bytes accessed | tf_op | source)
XLA Modules:
  0.0 19.3 jit_solution(6697973221055927666)
XLA Ops:
  0.0 16.4 %shard_map.100.padded_ref = f32[72,1280]{1,0:T(8,128)} custom-call(bf16[16,32,1024]{2,1,0:T(8,128)(2,1)} %gas_hbm.1, bf16[8,128]{1,0:T(8,128)(2,1)} %bitcast.11, s32[8,128]{1,0:T(8,128)} %bitcast.9, bf16[16,64]{1,0:T(8,128)(2,1)} %bitcast.10, f32[1,32]{1,0:T(1,128)} %bitcast.12, f32[32,128]{1,0:T(8,128)} %bitcast.7, f32[2,4096]{1,0:T(2,128)} %fine_albedo_ref.1, ...), custom_call_target="tpu_custom_call" | custom-call | tf_op jit(solution)/shard_map/pallas_call | solution.py:352
  16.4 2.8 %shard_map.101 = f32[33,2,1024]{2,1,0:T(2,128)} custom-call(f32[72,1280]{1,0:T(8,128)} %shard_map.100.padded_ref, s32[3,1024]{1,0:T(4,128)} %neighbours_ref.1, f32[3,1024]{1,0:T(4,128)} %weights_ref.1), custom_call_target="tpu_custom_call" | custom-call | tf_op jit(solution)/shard_map/pallas_call | solution.py:382
where the time goes:
time: 19.5 us; the launch traced here: 19.3 us
  Pallas kernels  19.3 us (99%)
    pallas_call x1, Pallas kernels, local(): pl.pallas_call(functools.partial(flux_kernel, n, span), out_shape=jax.Sha...  16.4 us
    pallas_call x1, Pallas kernels, local(): pl.pallas_call(side_kernel, out_shape=jax.ShapeDtypeStruct((lev + 1, 2, c...  2.82 us

commit v1 on v0

v1 whole, which is shorter than its diff:
```python
import functools
import math

import jax
import jax.numpy as jnp
from jax import lax
from jax.experimental import pallas as pl
from jax.experimental.pallas import tpu as pltpu
from jax.sharding import PartitionSpec as P

CB = 128
FB = 128
ASYM = 0.8
TAU_SCALE = 0.08
SSA_MAX = 0.98
LOG2E = math.log2(math.e)
CHUNK = 8
VMEM = pltpu.VMEM
GROUND = 2.0 / SSA_MAX - 1.0
DEPTH = 0.5 * TAU_SCALE * math.log(2.0) * SSA_MAX


def round_up(value, multiple):
    return -(-value // multiple) * multiple


def local_albedo(area_ref, albedo_ref, parent_ref, span):
    blocks = area_ref.shape[0]
    area = area_ref[...]
    rows = [
        jnp.concatenate([albedo_ref[s : s + 1, b * FB : (b + 1) * FB] for b in range(blocks)], axis=0)
        for s in range(2)
    ]
    weights = jnp.transpose(jnp.concatenate([area, area * rows[0], area * rows[1]], axis=0))
    parent = jnp.transpose(jnp.concatenate([parent_ref[...]] * 3, axis=0))
    inside = parent & (span - 1)
    totals = jnp.concatenate(
        [jnp.sum(jnp.where(inside == j, weights, 0.0), axis=0, keepdims=True) for j in range(span)], axis=0
    )
    share = totals[:, :blocks]
    first = (totals[:, blocks : 2 * blocks] / share).astype(jnp.bfloat16).astype(jnp.float32)
    second = (totals[:, 2 * blocks :] / share).astype(jnp.bfloat16).astype(jnp.float32)
    number = (parent[0:1, :blocks] // span).astype(jnp.float32)
    return first, second, number


def pick_albedo(pieces, start_span, span, blocks, ncb):
    per = CB // span
    table = jnp.concatenate(
        [jnp.concatenate([p[0:span, s * blocks : (s + 1) * blocks] for p in pieces], axis=1) for s in range(2)],
        axis=0,
    ).astype(jnp.bfloat16)
    number = jnp.concatenate([p[span : span + 1, 0:blocks] for p in pieces], axis=1).astype(jnp.int32)
    total = number.shape[1]
    row = lax.broadcasted_iota(jnp.int32, (ncb, total), 0) * per + start_span
    parts = []
    for m in range(per):
        chosen = (number == row + m).astype(jnp.float32).astype(jnp.bfloat16)
        parts.append(
            lax.dot_general(chosen, table, (((1,), (1,)), ((), ())), preferred_element_type=jnp.float32)
        )
    direct = jnp.concatenate([p[:, 0:span] for p in parts], axis=1)
    diffuse = jnp.concatenate([p[:, span : 2 * span] for p in parts], axis=1)
    return direct, diffuse


def expand_weight(weight_ref, big_ref):
    feats, rows = weight_ref.shape
    wide = big_ref.shape[1]
    source = lax.broadcasted_iota(jnp.int32, (feats, wide), 0)
    column = lax.broadcasted_iota(jnp.int32, (feats, wide), 1)
    spread = (column % (wide // 2) // CHUNK == source).astype(jnp.float32).astype(jnp.bfloat16)
    repeated = lax.dot_general(
        weight_ref[...], spread, (((0,), (0,)), ((), ())), preferred_element_type=jnp.float32
    )
    row = lax.broadcasted_iota(jnp.int32, (rows, wide), 0)
    place = lax.broadcasted_iota(jnp.int32, (rows, wide), 1)
    scaled = jnp.where(row < rows // 2, LOG2E * repeated, 0.5 * repeated)
    high = scaled.astype(jnp.bfloat16).astype(jnp.float32)
    scaled = jnp.where(place < wide // 2, high, scaled - high)
    level = place % CHUNK
    for l in range(CHUNK):
        big_ref[l * rows : (l + 1) * rows, :] = jnp.where(level == l, scaled, 0.0).astype(jnp.bfloat16)


def product(block, first, gas_ref, big_ref, mix_ref):
    feats = gas_ref.shape[0]
    cols = pl.ds(pl.multiple_of(block * CB, CB), CB)
    inputs = gas_ref[:, first : first + CHUNK, cols].reshape(feats * CHUNK, CB)
    mix_ref[...] = jnp.dot(
        big_ref[...], jnp.concatenate([inputs, inputs], axis=0), preferred_element_type=jnp.float32
    )


def layer(mix, rate, coef_ref, place):
    gpoints = mix.shape[0] // 2
    x = mix[:gpoints]
    soft = jnp.maximum(x, lax.log2(1.0 + jnp.exp2(jnp.minimum(x, 100.0))))
    u = jnp.tanh(mix[gpoints:])
    wide = 1.0 + u
    less = GROUND - u
    gap = 0.15 * wide
    more = less + gap
    square = less * more
    inverse = lax.rsqrt(square)
    bend = jnp.tanh(((square * inverse) * soft) * DEPTH)
    slope = bend * inverse
    total = (less + more) * slope
    bend2 = bend * bend
    plus = 1.0 + bend2
    coef_ref[0, place] = jnp.exp2(soft * rate)
    coef_ref[1, place] = wide
    coef_ref[2, place] = gap * slope
    coef_ref[3, place] = plus + total
    coef_ref[4, place] = plus - total
    coef_ref[5, place] = 1.0 - bend2


def recur(coef_ref, place, level, state_ref, back, fall, carry):
    direct, big_b, big_q = carry
    r, d, dd, t2 = [coef_ref[i, place] for i in range(2, 6)]
    below = direct * coef_ref[0, place]
    scattered = coef_ref[1, place] * (direct - below)
    rising = scattered * back
    falling = scattered * fall
    state_ref[2, level] = big_b
    state_ref[3, level] = big_q + direct
    z = 1.0 / (d - r * big_b)
    h = (big_q + big_b * rising) * z
    state_ref[0, level] = t2 * z
    state_ref[1, level] = r * h + rising
    return below, (r + dd * big_b) * z, t2 * h + falling


def fold(parts):
    place = lax.broadcasted_iota(jnp.int32, parts[0].shape, 0)
    distance = 1
    while len(parts) > 1:
        even = (place & distance) == 0
        parts = [
            jnp.where(even, p, q) + pltpu.roll(jnp.where(even, q, p), 8 - distance, 0)
            for p, q in zip(parts[0::2], parts[1::2])
        ]
        distance *= 2
    rest = parts[0]
    while distance < 8:
        rest = rest + pltpu.roll(rest, 8 - distance, 0)
        distance *= 2
    return rest


def gather_g(value):
    parts = [value[i : i + 8] for i in range(0, value.shape[0], 8)]
    while len(parts) > 1:
        parts = [p + q for p, q in zip(parts[0::2], parts[1::2])]
    return parts[0]


class Ascent:
    def __init__(self, cb, albedo_ref, lit_ref, state_ref, end_ref, flux_ref):
        lev = state_ref.shape[1]
        self.state_ref, self.flux_ref = state_ref, flux_ref
        self.lit = lit_ref[pl.ds(cb, 1), :]
        direct, big_b, big_q = end_ref[0], end_ref[1], end_ref[2]
        direct_albedo = albedo_ref[0, pl.ds(cb, 1), :]
        diffuse_albedo = albedo_ref[1, pl.ds(cb, 1), :]
        self.up = (diffuse_albedo * big_q + direct_albedo * direct) / (1.0 - diffuse_albedo * big_b)
        last = fold([gather_g(big_b * self.up + big_q + direct), gather_g(self.up)])
        flux_ref[2 * lev : 2 * lev + 8, :] = last * self.lit
        self.parts = []

    def level(self, level):
        state_ref = self.state_ref
        self.up = state_ref[0, level] * self.up + state_ref[1, level]
        down = state_ref[2, level] * self.up + state_ref[3, level]
        self.parts = [gather_g(down), gather_g(self.up)] + self.parts
        if level % 4 == 0:
            self.flux_ref[2 * level : 2 * level + 8, :] = fold(self.parts) * self.lit
            self.parts = []


def solar_column(solar_ref):
    row = solar_ref[...]
    n = row.shape[1]
    diagonal = lax.broadcasted_iota(jnp.int32, (n, n), 0) == lax.broadcasted_iota(jnp.int32, (n, n), 1)
    return jnp.sum(jnp.where(diagonal, row, 0.0), axis=1, keepdims=True)


def flux_kernel(
    n, span, gas_hbm, cos_ref, lit_ref, weight_ref, solar_ref, area_ref, fine_albedo_ref, parent_ref,
    flux_ref, big_ref, state_ref, end_ref, albedo_ref, cosf_ref, litf_ref, mine_ref, pieces_ref,
    edge_ref, halo_ref, mix_ref, early_ref, late_ref, gas_ref, send_sem, recv_sem, edge_send, edge_recv, gas_sem,
):
    ncb = cos_ref.shape[0]
    blocks = area_ref.shape[0]
    lev = gas_ref.shape[1]
    gpoints = solar_ref.shape[1]
    rows = 2 * gpoints
    half = lev // 2
    slots = state_ref.shape[0]
    me = lax.axis_index("blk")
    peers = [lax.rem(me + shift, n) for shift in range(1, n)]
    mesh_id = pl.DeviceIdType.MESH

    load = pltpu.make_async_copy(gas_hbm, gas_ref, gas_sem)
    load.start()
    barrier = pltpu.get_barrier_semaphore()
    for peer in peers:
        pl.semaphore_signal(barrier, inc=1, device_id={"blk": peer}, device_id_type=mesh_id)

    first, second, number = local_albedo(area_ref, fine_albedo_ref, parent_ref, span)
    mine_ref[...] = jnp.zeros_like(mine_ref)
    mine_ref[0:span, 0:blocks] = first
    mine_ref[0:span, blocks : 2 * blocks] = second
    mine_ref[span : span + 1, 0:blocks] = number
    expand_weight(weight_ref, big_ref)
    cosf_ref[...] = cos_ref[...].astype(jnp.float32)
    litf_ref[...] = lit_ref[...].astype(jnp.float32)
    solar = solar_column(solar_ref)

    def order(i):
        return jnp.where(i < 2, i * (ncb - 1), i - 1)

    def wide(row):
        return jnp.broadcast_to(row, (gpoints, CB))

    class Prepare:
        def __init__(self, cb, part, coef_ref):
            self.coef_ref = coef_ref
            self.part = part
            self.rate = wide((-TAU_SCALE) / cosf_ref[pl.ds(cb, 1), :])
            for turn in range(half // CHUNK):
                product(cb, part * half + turn * CHUNK, gas_ref, big_ref, mix_ref.at[part, turn])

        def level(self, place):
            turn, i = place // CHUNK, place % CHUNK
            mix = mix_ref[self.part, turn, i * rows : (i + 1) * rows, :]
            layer(mix, self.rate, self.coef_ref, place)

    coefs = (early_ref, late_ref)

    def ascent(i):
        cb = order(i)
        slot = lax.rem(i, slots)
        return Ascent(cb, albedo_ref, litf_ref, state_ref.at[slot], end_ref.at[slot], flux_ref.at[cb + 1])

    def step(i, ahead, ups):
        cb = order(i)
        slot = lax.rem(i, slots)
        mu = cosf_ref[pl.ds(cb, 1), :]
        back = (0.5 * (0.5 * SSA_MAX)) * (1.0 - ASYM * mu)
        fall = wide(0.5 * SSA_MAX - back)
        back = wide(back)
        zero = jnp.zeros((gpoints, CB), jnp.float32)
        carry = (solar * mu, zero, zero)
        ups = [ascent(j) for j in ups]
        for part in range(2):
            next_one = None
            if part == 0:
                next_one = Prepare(cb, 1, late_ref)
            elif ahead:
                next_one = Prepare(order(i + 1), 0, early_ref)
            for place in range(half):
                level = part * half + place
                for up in ups:
                    up.level(lev - 1 - level)
                carry = recur(coefs[part], place, level, state_ref.at[slot], back, fall, carry)
                if next_one is not None:
                    next_one.level(place)
        for j in range(3):
            end_ref[slot, j] = carry[j]

    load.wait()
    begin = Prepare(0, 0, early_ref)
    for place in range(half):
        begin.level(place)

    pl.semaphore_wait(barrier, n - 1)
    sends = []
    for i, peer in enumerate(peers):
        copy = pltpu.make_async_remote_copy(
            src_ref=mine_ref,
            dst_ref=pieces_ref.at[i],
            send_sem=send_sem.at[i],
            recv_sem=recv_sem.at[i],
            device_id={"blk": peer},
            device_id_type=mesh_id,
        )
        copy.start()
        sends.append(copy)

    def first_steps(i, unused):
        step(i, True, [])
        return unused

    lag = slots - 1
    lax.fori_loop(0, lag, first_steps, 0)
    for copy in sends:
        copy.wait()
    start_span = me * (ncb * CB // span)
    pieces = [mine_ref[...]] + [pieces_ref[i] for i in range(n - 1)]
    direct, diffuse = pick_albedo(pieces, start_span, span, blocks, ncb)
    albedo_ref[0] = direct
    albedo_ref[1] = diffuse

    edges = [
        pltpu.make_async_remote_copy(
            src_ref=edge_ref.at[i],
            dst_ref=halo_ref.at[i],
            send_sem=edge_send.at[i],
            recv_sem=edge_recv.at[i],
            device_id={"blk": peer},
            device_id_type=mesh_id,
        )
        for i, peer in ((0, peers[-1]), (1, peers[0]))
    ]

    def middle_steps(i, unused):
        step(i, True, [i - lag])

        @pl.when(i == lag + 1)
        def _():
            edge_ref[0] = flux_ref[1]
            edge_ref[1] = flux_ref[ncb]
            for copy in edges:
                copy.start()

        return unused

    lax.fori_loop(lag, ncb - 1, middle_steps, 0)
    step(ncb - 1, False, range(ncb - 1 - lag, ncb - 1))
    last = ascent(ncb - 1)
    for level in range(lev):
        last.level(lev - 1 - level)
    for copy in edges:
        copy.wait()
    flux_ref[0] = halo_ref[1]
    flux_ref[ncb + 1] = halo_ref[0]


def side_kernel(flux_ref, neighbours_ref, weights_ref, out_ref):
    interfaces, parts, cols = out_ref.shape
    ncb = cols // CB
    rows = flux_ref.shape[1]
    start = (lax.axis_index("grp") * lax.axis_size("blk") + lax.axis_index("blk")) * cols
    for cb in range(ncb):
        own = slice(cb * CB, (cb + 1) * CB)
        picked = neighbours_ref[:, own] - (start + (cb - 1) * CB)
        weights = weights_ref[:, own]
        lanes, blocks, shares = [], [], []
        for k in range(3):
            row = jnp.broadcast_to(picked[k : k + 1], (8, CB))
            lanes.append(row & (CB - 1))
            blocks.append(row // CB)
            shares.append(jnp.broadcast_to(weights[k : k + 1], (8, CB)))
        for r in range(0, rows, 8):
            near = [flux_ref[cb + j, r : r + 8, :] for j in range(3)]
            result = near[1]
            for k in range(3):
                before, here, after = [
                    jnp.take_along_axis(v, lanes[k], axis=1, mode="promise_in_bounds") for v in near
                ]
                beside = jnp.where(blocks[k] == 0, before, jnp.where(blocks[k] == 1, here, after))
                result = result + shares[k] * (beside - near[1])
            top = r // parts
            count = min(8 // parts, interfaces - top)
            out_ref[top : top + count, :, own] = result[: count * parts].reshape(count, parts, CB)


def local(
    gas_state, cos_zenith, daylit, fine_area, fine_albedo, parent_of,
    optics_weight, solar_weight, neighbours, side_weight,
):
    n = lax.axis_size("blk")
    feats, lev, cols = gas_state.shape
    gpoints = solar_weight.shape[0]
    ncb = cols // CB
    blocks = fine_area.shape[0] // FB
    span = cols // blocks
    rows = round_up(2 * (lev + 1), 8)
    half = lev // 2
    slots = 3
    full = pl.BlockSpec(memory_space=VMEM)
    coef = VMEM((6, half, gpoints, CB), jnp.float32)
    fluxes = pl.pallas_call(
        functools.partial(flux_kernel, n, span),
        out_shape=jax.ShapeDtypeStruct((ncb + 2, rows, CB), jnp.float32),
        in_specs=[pl.BlockSpec(memory_space=pltpu.HBM)] + [full] * 7,
        out_specs=full,
        scratch_shapes=[
            VMEM((CHUNK * 2 * gpoints, 2 * CHUNK * feats), jnp.bfloat16),
            VMEM((slots, 4, lev, gpoints, CB), jnp.float32),
            VMEM((slots, 3, gpoints, CB), jnp.float32),
            VMEM((2, ncb, CB), jnp.float32),
            VMEM((ncb, CB), jnp.float32),
            VMEM((ncb, CB), jnp.float32),
            VMEM((span + 8, 128), jnp.float32),
            VMEM((n - 1, span + 8, 128), jnp.float32),
            VMEM((2, rows, CB), jnp.float32),
            VMEM((2, rows, CB), jnp.float32),
            VMEM((2, half // CHUNK, CHUNK * 2 * gpoints, CB), jnp.float32),
            coef,
            coef,
            VMEM((feats, lev, cols), gas_state.dtype),
            pltpu.SemaphoreType.DMA((n - 1,)),
            pltpu.SemaphoreType.DMA((n - 1,)),
            pltpu.SemaphoreType.DMA((2,)),
            pltpu.SemaphoreType.DMA((2,)),
            pltpu.SemaphoreType.DMA,
        ],
        compiler_params=pltpu.CompilerParams(
            collective_id=0, has_side_effects=True, vmem_limit_bytes=24 << 20
        ),
    )(
        gas_state, cos_zenith.reshape(ncb, CB), daylit.reshape(ncb, CB), optics_weight.T,
        solar_weight.reshape(1, gpoints), fine_area.reshape(blocks, FB), fine_albedo,
        parent_of.reshape(blocks, FB),
    )
    result = pl.pallas_call(
        side_kernel,
        out_shape=jax.ShapeDtypeStruct((lev + 1, 2, cols), jnp.float32),
        in_specs=[full] * 3,
        out_specs=full,
        compiler_params=pltpu.CompilerParams(vmem_limit_bytes=8 << 20),
    )(fluxes, neighbours, side_weight)
    return jnp.transpose(result, (1, 0, 2))


def solution(mesh):
    columns = P(("grp", "blk"))
    last = P(None, ("grp", "blk"))
    in_specs = (
        P(None, None, ("grp", "blk")), columns, columns, columns, last, columns, P(), P(), last, last,
    )
    out_specs = P(None, None, ("grp", "blk"))
    return jax.shard_map(local, mesh=mesh, in_specs=in_specs, out_specs=out_specs, check_vma=False)
```

time: 19.5 us -> 21.1 us (1.082)
  local copies, waits for them, and re-layouts: 0 us -> 4.14 us
  Pallas kernels: 19.3 us -> 16.6 us
    unnamed x0 -> x20, local copies, waits for them, and re-layouts: none -> 4.14 us
    pallas_call x1, Pallas kernels: 16.4 us -> 14.4 us  [local(): pl.pallas_call(functools.partial(flux_kernel, n, span), out_shape=jax.Sha...]
    pallas_call x1, Pallas kernels: 2.82 us -> 2.15 us  [local(): pl.pallas_call(side_kernel, out_shape=jax.ShapeDtypeStruct((lev + 1, 2, c...]
where the time goes in v1:
time: 21.1 us; the launch traced here: 20.8 us
  Pallas kernels  16.6 us (79%)
  local copies, waits for them, and re-layouts  4.14 us (20%)
    pallas_call x1, Pallas kernels, local(): pl.pallas_call(functools.partial(flux_kernel, n, span), out_shape=jax.Sha...  14.4 us
    unnamed x20, local copies, waits for them, and re-layouts  4.14 us
    pallas_call x1, Pallas kernels, local(): pl.pallas_call(side_kernel, out_shape=jax.ShapeDtypeStruct((lev + 1, 2, c...  2.15 us

profile of v1, /device:TPU:0, one launch (start us, length us, event | category | flops | bytes accessed | tf_op | source)
XLA Modules:
  0.0 20.8 jit_solution(3351071801220237728)
XLA Ops:
  0.0 0.0 copy-start.8
  0.0 0.0 copy-start.7
  0.0 0.0 copy-start.6
  0.0 0.0 copy-start.9
  0.0 0.7 %copy-done.8 = bf16[1024]{0:T(1024)(128)(2,1)S(1)} copy-done((bf16[1024]{0:T(1024)(128)(2,1)S(1)}, bf16[1024]{0:T(1024)(128)(2,1)}, u32[]{:S(2)}) %copy-start.8) | copy-done | bytes 2072
  0.7 0.0 copy-done.7
  0.7 0.0 copy-done.6
  0.7 0.0 copy-done.9
  0.7 0.0 copy-start
  0.7 1.2 %copy-done = bf16[16,32,1024]{2,1,0:T(8,128)(2,1)S(1)} copy-done((bf16[16,32,1024]{2,1,0:T(8,128)(2,1)S(1)}, bf16[16,32,1024]{2,1,0:T(8,128)(2,1)}, u32[]{:S(2)}) %copy-start) | copy-done | bytes 1048600
  1.9 0.0 copy-start.1
  1.9 0.8 %copy-done.1 = f32[2,4096]{1,0:T(2,128)S(1)} copy-done((f32[2,4096]{1,0:T(2,128)S(1)}, f32[2,4096]{1,0:T(2,128)}, u32[]{:S(2)}) %copy-start.1) | copy-done | bytes 32792
  2.7 0.0 copy-start.2
  2.7 0.7 %copy-done.2 = f32[4096]{0:T(1024)S(1)} copy-done((f32[4096]{0:T(1024)S(1)}, f32[4096]{0:T(1024)}, u32[]{:S(2)}) %copy-start.2) | copy-done | bytes 16408
  3.4 0.0 copy-start.3
  3.4 0.7 %copy-done.3 = s32[4096]{0:T(1024)S(1)} copy-done((s32[4096]{0:T(1024)S(1)}, s32[4096]{0:T(1024)}, u32[]{:S(2)}) %copy-start.3) | copy-done | bytes 16408
  4.1 0.0 copy-start.4
  4.1 0.0 copy-start.5
  4.1 14.4 %shard_map.100.flux_ref = f32[10,72,128]{2,1,0:T(8,128)S(1)} custom-call(bf16[16,32,1024]{2,1,0:T(8,128)(2,1)S(1)} %copy-done, bf16[8,128]{1,0:T(8,128)(2,1)S(1)} %bitcast.11, s32[8,128]{1,0:T(8,128)S(1)} %bitcast.9, bf16[16,64]{1,0:T(8,128)(2,1)S(1)} %bitcast.10, f32[1,32]{1,0:T(1,128)S(1)} %bitcast.12, f32[32,128]{1,0:T(8,128)S(1)} %bitcast.7, ...), custom_call_target="tpu_custom_call" | custom-call | tf_op jit(solution)/shard_map/pallas_call | solution.py:385
  18.6 0.0 copy-done.4
  18.6 0.0 copy-done.5
  18.6 2.2 %shard_map.101 = f32[33,2,1024]{2,1,0:T(2,128)} custom-call(f32[10,72,128]{2,1,0:T(8,128)S(1)} %shard_map.100.flux_ref, s32[3,1024]{1,0:T(4,128)S(1)} %copy-done.4, f32[3,1024]{1,0:T(4,128)S(1)} %copy-done.5), custom_call_target="tpu_custom_call" | custom-call | tf_op jit(solution)/shard_map/pallas_call | solution.py:419
Async XLA Ops:
  0.0 0.7 %copy-start.8 = (bf16[1024]{0:T(1024)(128)(2,1)S(1)}, bf16[1024]{0:T(1024)(128)(2,1)}, u32[]{:S(2)}) copy-start(bf16[1024]{0:T(1024)(128)(2,1)} %param.11) | copy-start | bytes 6148
  0.0 0.7 %copy-start.7 = (bf16[64,16]{0,1:T(8,128)(2,1)S(1)}, bf16[64,16]{0,1:T(8,128)(2,1)}, u32[]{:S(2)}) copy-start(bf16[64,16]{0,1:T(8,128)(2,1)} %param.16) | copy-start | bytes 6148
  0.0 0.7 %copy-start.6 = (s32[1024]{0:T(1024)S(1)}, s32[1024]{0:T(1024)}, u32[]{:S(2)}) copy-start(s32[1024]{0:T(1024)} %param.12) | copy-start | bytes 12292
  0.0 0.7 %copy-start.9 = (f32[32]{0:T(128)S(1)}, f32[32]{0:T(128)}, u32[]{:S(2)}) copy-start(f32[32]{0:T(128)} %param.17) | copy-start | bytes 388
  0.7 1.2 %copy-start = (bf16[16,32,1024]{2,1,0:T(8,128)(2,1)S(1)}, bf16[16,32,1024]{2,1,0:T(8,128)(2,1)}, u32[]{:S(2)}) copy-start(bf16[16,32,1024]{2,1,0:T(8,128)(2,1)} %gas_hbm.1) | copy-start | bytes 3145732
  1.9 0.8 %copy-start.1 = (f32[2,4096]{1,0:T(2,128)S(1)}, f32[2,4096]{1,0:T(2,128)}, u32[]{:S(2)}) copy-start(f32[2,4096]{1,0:T(2,128)} %fine_albedo_ref.1) | copy-start | bytes 98308
  2.7 0.7 %copy-start.2 = (f32[4096]{0:T(1024)S(1)}, f32[4096]{0:T(1024)}, u32[]{:S(2)}) copy-start(f32[4096]{0:T(1024)} %param.13) | copy-start | bytes 49156
  3.4 0.7 %copy-start.3 = (s32[4096]{0:T(1024)S(1)}, s32[4096]{0:T(1024)}, u32[]{:S(2)}) copy-start(s32[4096]{0:T(1024)} %param.15) | copy-start | bytes 49156
  4.1 14.5 %copy-start.4 = (s32[3,1024]{1,0:T(4,128)S(1)}, s32[3,1024]{1,0:T(4,128)}, u32[]{:S(2)}) copy-start(s32[3,1024]{1,0:T(4,128)} %neighbours_ref.1) | copy-start | bytes 36868
  4.1 14.5 %copy-start.5 = (f32[3,1024]{1,0:T(4,128)S(1)}, f32[3,1024]{1,0:T(4,128)}, u32[]{:S(2)}) copy-start(f32[3,1024]{1,0:T(4,128)} %weights_ref.1) | copy-start | bytes 36868

commit v2 on v1

--- a/solution.py
+++ b/solution.py
@@ -83,10 +83,20 @@
         big_ref[l * rows : (l + 1) * rows, :] = jnp.where(level == l, scaled, 0.0).astype(jnp.bfloat16)
 
 
-def product(block, first, gas_ref, big_ref, mix_ref):
+def stage(block, first, gas_ref, inputs_ref):
     feats = gas_ref.shape[0]
     cols = pl.ds(pl.multiple_of(block * CB, CB), CB)
-    inputs = gas_ref[:, first : first + CHUNK, cols].reshape(feats * CHUNK, CB)
+    inputs_ref[...] = jnp.concatenate(
+        [
+            gas_ref[:, level : level + CHUNK, cols].reshape(feats * CHUNK, CB)
+            for level in (first, first + CHUNK)
+        ],
+        axis=1,
+    )
+
+
+def product(inputs_ref, big_ref, mix_ref):
+    inputs = inputs_ref[...]
     mix_ref[...] = jnp.dot(
         big_ref[...], jnp.concatenate([inputs, inputs], axis=0), preferred_element_type=jnp.float32
     )
@@ -116,7 +126,7 @@
     coef_ref[5, place] = 1.0 - bend2
 
 
-def recur(coef_ref, place, level, state_ref, back, fall, carry):
+def recur(coef_ref, place, state_ref, level, back, fall, carry):
     direct, big_b, big_q = carry
     r, d, dd, t2 = [coef_ref[i, place] for i in range(2, 6)]
     below = direct * coef_ref[0, place]
@@ -157,16 +167,13 @@
 
 
 class Ascent:
-    def __init__(self, cb, albedo_ref, lit_ref, state_ref, end_ref, flux_ref):
+    def __init__(self, albedo, lit, carry, state_ref, rise_ref):
         lev = state_ref.shape[1]
-        self.state_ref, self.flux_ref = state_ref, flux_ref
-        self.lit = lit_ref[pl.ds(cb, 1), :]
-        direct, big_b, big_q = end_ref[0], end_ref[1], end_ref[2]
-        direct_albedo = albedo_ref[0, pl.ds(cb, 1), :]
-        diffuse_albedo = albedo_ref[1, pl.ds(cb, 1), :]
-        self.up = (diffuse_albedo * big_q + direct_albedo * direct) / (1.0 - diffuse_albedo * big_b)
+        self.state_ref, self.rise_ref, self.lit = state_ref, rise_ref, lit
+        direct, big_b, big_q = carry
+        self.up = (albedo[1] * big_q + albedo[0] * direct) / (1.0 - albedo[1] * big_b)
         last = fold([gather_g(big_b * self.up + big_q + direct), gather_g(self.up)])
-        flux_ref[2 * lev : 2 * lev + 8, :] = last * self.lit
+        rise_ref[2 * lev : 2 * lev + 8, :] = last * lit
         self.parts = []
 
     def level(self, level):
@@ -175,7 +182,7 @@
         down = state_ref[2, level] * self.up + state_ref[3, level]
         self.parts = [gather_g(down), gather_g(self.up)] + self.parts
         if level % 4 == 0:
-            self.flux_ref[2 * level : 2 * level + 8, :] = fold(self.parts) * self.lit
+            self.rise_ref[2 * level : 2 * level + 8, :] = fold(self.parts) * self.lit
             self.parts = []
 
 
@@ -188,16 +195,14 @@
 
 def flux_kernel(
     n, span, gas_hbm, cos_ref, lit_ref, weight_ref, solar_ref, area_ref, fine_albedo_ref, parent_ref,
-    flux_ref, big_ref, state_ref, end_ref, albedo_ref, cosf_ref, litf_ref, mine_ref, pieces_ref,
-    edge_ref, halo_ref, mix_ref, early_ref, late_ref, gas_ref, send_sem, recv_sem, edge_send, edge_recv, gas_sem,
+    flux_ref, big_ref, state_ref, first_ref, end_ref, albedo_ref, cosf_ref, litf_ref, mine_ref, pieces_ref,
+    edge_ref, halo_ref, inputs_ref, mix_ref, next_ref, coef_ref, rise_ref, gas_ref, send_sem, recv_sem, edge_send, edge_recv, gas_sem,
 ):
     ncb = cos_ref.shape[0]
     blocks = area_ref.shape[0]
     lev = gas_ref.shape[1]
     gpoints = solar_ref.shape[1]
     rows = 2 * gpoints
-    half = lev // 2
-    slots = state_ref.shape[0]
     me = lax.axis_index("blk")
     peers = [lax.rem(me + shift, n) for shift in range(1, n)]
     mesh_id = pl.DeviceIdType.MESH
@@ -219,61 +224,74 @@
     solar = solar_column(solar_ref)
 
     def order(i):
+        if isinstance(i, int):
+            return i * (ncb - 1) if i < 2 else i - 1
         return jnp.where(i < 2, i * (ncb - 1), i - 1)
 
     def wide(row):
         return jnp.broadcast_to(row, (gpoints, CB))
 
+    def rate_of(cb):
+        return wide((-TAU_SCALE) / cosf_ref[pl.ds(cb, 1), :])
+
+    def stage_pair(cb, pair):
+        stage(cb, 2 * pair * CHUNK, gas_ref, inputs_ref.at[pair])
+
+    def multiply(cb, target_ref):
+        for pair in range(2):
+            stage_pair(cb, pair)
+            product(inputs_ref.at[pair], big_ref, target_ref.at[pair])
+
     class Prepare:
-        def __init__(self, cb, part, coef_ref):
-            self.coef_ref = coef_ref
-            self.part = part
-            self.rate = wide((-TAU_SCALE) / cosf_ref[pl.ds(cb, 1), :])
-            for turn in range(half // CHUNK):
-                product(cb, part * half + turn * CHUNK, gas_ref, big_ref, mix_ref.at[part, turn])
-
-        def level(self, place):
-            turn, i = place // CHUNK, place % CHUNK
-            mix = mix_ref[self.part, turn, i * rows : (i + 1) * rows, :]
-            layer(mix, self.rate, self.coef_ref, place)
-
-    coefs = (early_ref, late_ref)
-
-    def ascent(i):
+        def __init__(self, rate):
+            self.rate, self.done = rate, 0
+
+        def until(self, count):
+            for level in range(self.done, int(count)):
+                chunk, i = level // CHUNK, level % CHUNK
+                left = chunk % 2 * CB
+                mix = mix_ref[chunk // 2, i * rows : (i + 1) * rows, left : left + CB]
+                layer(mix, self.rate, coef_ref, level)
+            self.done = max(self.done, int(count))
+
+    def step(i, ahead, state_ref, ascend=True, pending=None):
         cb = order(i)
-        slot = lax.rem(i, slots)
-        return Ascent(cb, albedo_ref, litf_ref, state_ref.at[slot], end_ref.at[slot], flux_ref.at[cb + 1])
-
-    def step(i, ahead, ups):
-        cb = order(i)
-        slot = lax.rem(i, slots)
         mu = cosf_ref[pl.ds(cb, 1), :]
         back = (0.5 * (0.5 * SSA_MAX)) * (1.0 - ASYM * mu)
         fall = wide(0.5 * SSA_MAX - back)
         back = wide(back)
         zero = jnp.zeros((gpoints, CB), jnp.float32)
         carry = (solar * mu, zero, zero)
-        ups = [ascent(j) for j in ups]
-        for part in range(2):
-            next_one = None
-            if part == 0:
-                next_one = Prepare(cb, 1, late_ref)
-            elif ahead:
-                next_one = Prepare(order(i + 1), 0, early_ref)
-            for place in range(half):
-                level = part * half + place
-                for up in ups:
-                    up.level(lev - 1 - level)
-                carry = recur(coefs[part], place, level, state_ref.at[slot], back, fall, carry)
-                if next_one is not None:
-                    next_one.level(place)
-        for j in range(3):
-            end_ref[slot, j] = carry[j]
-
-    load.wait()
-    begin = Prepare(0, 0, early_ref)
-    for place in range(half):
-        begin.level(place)
+        lit = litf_ref[pl.ds(cb, 1), :]
+        if ascend:
+            albedo = [albedo_ref[s, pl.ds(cb, 1), :] for s in range(2)]
+        following = None
+        if ahead:
+            following = Prepare(rate_of(order(i + 1)))
+            later = not isinstance(i, int) or i + 2 < ncb
+            if later:
+                for pair in range(2):
+                    stage_pair(order(jnp.minimum(i + 2, ncb - 1)), pair)
+                for pair in range(2):
+                    product(inputs_ref.at[pair], big_ref, next_ref.at[pair])
+        share = 0.78 if ascend else 1.0
+        for level in range(lev):
+            if pending is not None:
+                pending.level(lev - 1 - level)
+            carry = recur(coef_ref, level, state_ref, level, back, fall, carry)
+            if following is not None:
+                following.until(share * (level + 1))
+        if not ascend:
+            mix_ref[...] = next_ref[...]
+            return carry
+        up = Ascent(albedo, lit, carry, state_ref, rise_ref.at[0])
+        for level in range(lev):
+            up.level(lev - 1 - level)
+            if following is not None:
+                following.until(lev * (share + (1.0 - share) * (level + 1) / lev) + 1e-6)
+        if following is not None and later:
+            mix_ref[...] = next_ref[...]
+        flux_ref[cb + 1] = rise_ref[0]
 
     pl.semaphore_wait(barrier, n - 1)
     sends = []
@@ -289,12 +307,14 @@
         copy.start()
         sends.append(copy)
 
-    def first_steps(i, unused):
-        step(i, True, [])
-        return unused
-
-    lag = slots - 1
-    lax.fori_loop(0, lag, first_steps, 0)
+    load.wait()
+    multiply(0, mix_ref)
+    Prepare(rate_of(0)).until(lev)
+    multiply(order(1), mix_ref)
+    carry = step(0, True, first_ref, ascend=False)
+    for i in range(3):
+        end_ref[i] = carry[i]
+
     for copy in sends:
         copy.wait()
     start_span = me * (ncb * CB // span)
@@ -302,9 +322,17 @@
     direct, diffuse = pick_albedo(pieces, start_span, span, blocks, ncb)
     albedo_ref[0] = direct
     albedo_ref[1] = diffuse
-
-    edges = [
-        pltpu.make_async_remote_copy(
+    pending = Ascent(
+        [albedo_ref[s, 0:1, :] for s in range(2)], litf_ref[0:1, :], [end_ref[i] for i in range(3)],
+        first_ref, rise_ref.at[1],
+    )
+    step(1, True, state_ref, pending=pending)
+    flux_ref[1] = rise_ref[1]
+    edge_ref[0] = rise_ref[1]
+    edge_ref[1] = rise_ref[0]
+    sends = []
+    for i, peer in ((0, peers[-1]), (1, peers[0])):
+        copy = pltpu.make_async_remote_copy(
             src_ref=edge_ref.at[i],
             dst_ref=halo_ref.at[i],
             send_sem=edge_send.at[i],
@@ -312,27 +340,16 @@
             device_id={"blk": peer},
             device_id_type=mesh_id,
         )
-        for i, peer in ((0, peers[-1]), (1, peers[0]))
-    ]
+        copy.start()
+        sends.append(copy)
 
     def middle_steps(i, unused):
-        step(i, True, [i - lag])
-
-        @pl.when(i == lag + 1)
-        def _():
-            edge_ref[0] = flux_ref[1]
-            edge_ref[1] = flux_ref[ncb]
-            for copy in edges:
-                copy.start()
-
+        step(i, True, state_ref)
         return unused
 
-    lax.fori_loop(lag, ncb - 1, middle_steps, 0)
-    step(ncb - 1, False, range(ncb - 1 - lag, ncb - 1))
-    last = ascent(ncb - 1)
-    for level in range(lev):
-        last.level(lev - 1 - level)
-    for copy in edges:
+    lax.fori_loop(2, ncb - 1, middle_steps, 0)
+    step(ncb - 1, False, state_ref)
+    for copy in sends:
         copy.wait()
     flux_ref[0] = halo_ref[1]
     flux_ref[ncb + 1] = halo_ref[0]
@@ -353,15 +370,16 @@
             lanes.append(row & (CB - 1))
             blocks.append(row // CB)
             shares.append(jnp.broadcast_to(weights[k : k + 1], (8, CB)))
-        for r in range(0, rows, 8):
-            near = [flux_ref[cb + j, r : r + 8, :] for j in range(3)]
-            result = near[1]
-            for k in range(3):
+        results = [flux_ref[cb + 1, r : r + 8, :] for r in range(0, rows, 8)]
+        for k in range(3):
+            for i, r in enumerate(range(0, rows, 8)):
+                near = [flux_ref[cb + j, r : r + 8, :] for j in range(3)]
                 before, here, after = [
                     jnp.take_along_axis(v, lanes[k], axis=1, mode="promise_in_bounds") for v in near
                 ]
                 beside = jnp.where(blocks[k] == 0, before, jnp.where(blocks[k] == 1, here, after))
-                result = result + shares[k] * (beside - near[1])
+                results[i] = results[i] + shares[k] * (beside - near[1])
+        for r, result in zip(range(0, rows, 8), results):
             top = r // parts
             count = min(8 // parts, interfaces - top)
             out_ref[top : top + count, :, own] = result[: count * parts].reshape(count, parts, CB)
@@ -378,10 +396,8 @@
     blocks = fine_area.shape[0] // FB
     span = cols // blocks
     rows = round_up(2 * (lev + 1), 8)
-    half = lev // 2
-    slots = 3
     full = pl.BlockSpec(memory_space=VMEM)
-    coef = VMEM((6, half, gpoints, CB), jnp.float32)
+    state = VMEM((4, lev, gpoints, CB), jnp.float32)
     fluxes = pl.pallas_call(
         functools.partial(flux_kernel, n, span),
         out_shape=jax.ShapeDtypeStruct((ncb + 2, rows, CB), jnp.float32),
@@ -389,8 +405,9 @@
         out_specs=full,
         scratch_shapes=[
             VMEM((CHUNK * 2 * gpoints, 2 * CHUNK * feats), jnp.bfloat16),
-            VMEM((slots, 4, lev, gpoints, CB), jnp.float32),
-            VMEM((slots, 3, gpoints, CB), jnp.float32),
+            state,
+            state,
+            VMEM((3, gpoints, CB), jnp.float32),
             VMEM((2, ncb, CB), jnp.float32),
             VMEM((ncb, CB), jnp.float32),
             VMEM((ncb, CB), jnp.float32),
@@ -398,9 +415,11 @@
             VMEM((n - 1, span + 8, 128), jnp.float32),
             VMEM((2, rows, CB), jnp.float32),
             VMEM((2, rows, CB), jnp.float32),
-            VMEM((2, half // CHUNK, CHUNK * 2 * gpoints, CB), jnp.float32),
-            coef,
-            coef,
+            VMEM((2, CHUNK * feats, 2 * CB), gas_state.dtype),
+            VMEM((2, CHUNK * 2 * gpoints, 2 * CB), jnp.float32),
+            VMEM((2, CHUNK * 2 * gpoints, 2 * CB), jnp.float32),
+            VMEM((6, lev, gpoints, CB), jnp.float32),
+            VMEM((2, rows, CB), jnp.float32),
             VMEM((feats, lev, cols), gas_state.dtype),
             pltpu.SemaphoreType.DMA((n - 1,)),
             pltpu.SemaphoreType.DMA((n - 1,)),
@@ -411,11 +430,14 @@
         compiler_params=pltpu.CompilerParams(
             collective_id=0, has_side_effects=True, vmem_limit_bytes=24 << 20
         ),
-    )(
-        gas_state, cos_zenith.reshape(ncb, CB), daylit.reshape(ncb, CB), optics_weight.T,
-        solar_weight.reshape(1, gpoints), fine_area.reshape(blocks, FB), fine_albedo,
-        parent_of.reshape(blocks, FB),
-    )
+    )(*[
+        pltpu.with_memory_space_constraint(value, pltpu.HBM)
+        for value in (
+            gas_state, cos_zenith.reshape(ncb, CB), daylit.reshape(ncb, CB), optics_weight.T,
+            solar_weight.reshape(1, gpoints), fine_area.reshape(blocks, FB), fine_albedo,
+            parent_of.reshape(blocks, FB),
+        )
+    ])
     result = pl.pallas_call(
         side_kernel,
         out_shape=jax.ShapeDtypeStruct((lev + 1, 2, cols), jnp.float32),

time: 21.1 us -> 16.6 us (0.79)
  local copies, waits for them, and re-layouts: 4.14 us -> 0.01 us
  Pallas kernels: 16.6 us -> 16.3 us
    unnamed x20 -> x4, local copies, waits for them, and re-layouts: 4.14 us -> 0.01 us
    pallas_call x1, Pallas kernels: 2.15 us -> 1.55 us  [local(): pl.pallas_call(side_kernel, out_shape=jax.ShapeDtypeStruct((lev + 1, 2, c...]
    pallas_call x1, Pallas kernels: 14.4 us -> 14.8 us  [local(): pl.pallas_call(functools.partial(flux_kernel, n, span), out_shape=jax.Sha...]
where the time goes in v2:
time: 16.6 us; the launch traced here: 16.4 us
  Pallas kernels  16.3 us (98%)
    pallas_call x1, Pallas kernels, local(): pl.pallas_call(functools.partial(flux_kernel, n, span), out_shape=jax.Sha...  14.8 us
    pallas_call x1, Pallas kernels, local(): pl.pallas_call(side_kernel, out_shape=jax.ShapeDtypeStruct((lev + 1, 2, c...  1.55 us

profile of v2, /device:TPU:0, one launch (start us, length us, event | category | flops | bytes accessed | tf_op | source)
XLA Modules:
  0.0 16.4 jit_solution(4865522235980751244)
XLA Ops:
  0.0 0.0 copy-start
  0.0 0.0 copy-start.1
  0.0 14.8 %shard_map.100.flux_ref = f32[10,72,128]{2,1,0:T(8,128)S(1)} custom-call(bf16[16,32,1024]{2,1,0:T(8,128)(2,1)} %gas_hbm.1, bf16[8,128]{1,0:T(8,128)(2,1)} %bitcast.11, s32[8,128]{1,0:T(8,128)} %bitcast.9, bf16[16,64]{1,0:T(8,128)(2,1)} %bitcast.10, f32[1,32]{1,0:T(1,128)} %bitcast.12, f32[32,128]{1,0:T(8,128)} %bitcast.7, f32[2,4096]{1,0:T(2,128)} %fine_albedo_ref.1, ...), custom_call_target="tpu_custom_call" | custom-call | tf_op jit(solution)/shard_map/pallas_call | solution.py:401
  14.8 0.0 copy-done
  14.8 0.0 copy-done.1
  14.8 1.6 %shard_map.101 = f32[33,2,1024]{2,1,0:T(2,128)} custom-call(f32[10,72,128]{2,1,0:T(8,128)S(1)} %shard_map.100.flux_ref, s32[3,1024]{1,0:T(4,128)S(1)} %copy-done, f32[3,1024]{1,0:T(4,128)S(1)} %copy-done.1), custom_call_target="tpu_custom_call" | custom-call | tf_op jit(solution)/shard_map/pallas_call | solution.py:441
Async XLA Ops:
  0.0 14.8 %copy-start = (s32[3,1024]{1,0:T(4,128)S(1)}, s32[3,1024]{1,0:T(4,128)}, u32[]{:S(2)}) copy-start(s32[3,1024]{1,0:T(4,128)} %neighbours_ref.1) | copy-start | bytes 36868
  0.0 14.8 %copy-start.1 = (f32[3,1024]{1,0:T(4,128)S(1)}, f32[3,1024]{1,0:T(4,128)}, u32[]{:S(2)}) copy-start(f32[3,1024]{1,0:T(4,128)} %weights_ref.1) | copy-start | bytes 36868

commit v3 on v2

--- a/solution.py
+++ b/solution.py
@@ -102,44 +102,36 @@
     )
 
 
-def layer(mix, rate, coef_ref, place):
+def layer(mix, rate, back, fall, carry, state_ref, level):
     gpoints = mix.shape[0] // 2
+    direct, big_b, big_q = carry
     x = mix[:gpoints]
     soft = jnp.maximum(x, lax.log2(1.0 + jnp.exp2(jnp.minimum(x, 100.0))))
+    below = direct * jnp.exp2(soft * rate)
     u = jnp.tanh(mix[gpoints:])
     wide = 1.0 + u
     less = GROUND - u
-    gap = 0.15 * wide
+    gap = (0.75 * (1.0 - ASYM)) * wide
     more = less + gap
     square = less * more
     inverse = lax.rsqrt(square)
     bend = jnp.tanh(((square * inverse) * soft) * DEPTH)
     slope = bend * inverse
     total = (less + more) * slope
+    r = gap * slope
     bend2 = bend * bend
     plus = 1.0 + bend2
-    coef_ref[0, place] = jnp.exp2(soft * rate)
-    coef_ref[1, place] = wide
-    coef_ref[2, place] = gap * slope
-    coef_ref[3, place] = plus + total
-    coef_ref[4, place] = plus - total
-    coef_ref[5, place] = 1.0 - bend2
-
-
-def recur(coef_ref, place, state_ref, level, back, fall, carry):
-    direct, big_b, big_q = carry
-    r, d, dd, t2 = [coef_ref[i, place] for i in range(2, 6)]
-    below = direct * coef_ref[0, place]
-    scattered = coef_ref[1, place] * (direct - below)
+    scattered = wide * (direct - below)
     rising = scattered * back
     falling = scattered * fall
     state_ref[2, level] = big_b
     state_ref[3, level] = big_q + direct
-    z = 1.0 / (d - r * big_b)
+    z = 1.0 / ((plus + total) - r * big_b)
     h = (big_q + big_b * rising) * z
+    t2 = 1.0 - bend2
     state_ref[0, level] = t2 * z
     state_ref[1, level] = r * h + rising
-    return below, (r + dd * big_b) * z, t2 * h + falling
+    return below, (r + (plus - total) * big_b) * z, t2 * h + falling
 
 
 def fold(parts):
@@ -195,14 +187,15 @@
 
 def flux_kernel(
     n, span, gas_hbm, cos_ref, lit_ref, weight_ref, solar_ref, area_ref, fine_albedo_ref, parent_ref,
-    flux_ref, big_ref, state_ref, first_ref, end_ref, albedo_ref, cosf_ref, litf_ref, mine_ref, pieces_ref,
-    edge_ref, halo_ref, inputs_ref, mix_ref, next_ref, coef_ref, rise_ref, gas_ref, send_sem, recv_sem, edge_send, edge_recv, gas_sem,
+    flux_ref, big_ref, states_ref, end_ref, albedo_ref, cosf_ref, litf_ref, mine_ref, pieces_ref,
+    edge_ref, halo_ref, inputs_ref, mix_ref, next_ref, gas_ref, send_sem, recv_sem, edge_send, edge_recv, gas_sem,
 ):
     ncb = cos_ref.shape[0]
     blocks = area_ref.shape[0]
     lev = gas_ref.shape[1]
     gpoints = solar_ref.shape[1]
     rows = 2 * gpoints
+    slots = states_ref.shape[0]
     me = lax.axis_index("blk")
     peers = [lax.rem(me + shift, n) for shift in range(1, n)]
     mesh_id = pl.DeviceIdType.MESH
@@ -231,68 +224,48 @@
     def wide(row):
         return jnp.broadcast_to(row, (gpoints, CB))
 
-    def rate_of(cb):
-        return wide((-TAU_SCALE) / cosf_ref[pl.ds(cb, 1), :])
-
     def stage_pair(cb, pair):
         stage(cb, 2 * pair * CHUNK, gas_ref, inputs_ref.at[pair])
 
-    def multiply(cb, target_ref):
-        for pair in range(2):
-            stage_pair(cb, pair)
-            product(inputs_ref.at[pair], big_ref, target_ref.at[pair])
-
-    class Prepare:
-        def __init__(self, rate):
-            self.rate, self.done = rate, 0
-
-        def until(self, count):
-            for level in range(self.done, int(count)):
-                chunk, i = level // CHUNK, level % CHUNK
-                left = chunk % 2 * CB
-                mix = mix_ref[chunk // 2, i * rows : (i + 1) * rows, left : left + CB]
-                layer(mix, self.rate, coef_ref, level)
-            self.done = max(self.done, int(count))
-
-    def step(i, ahead, state_ref, ascend=True, pending=None):
+    def down(i, mix_ref, next_ref):
         cb = order(i)
+        slot = lax.rem(i, slots)
+        state_ref = states_ref.at[slot]
         mu = cosf_ref[pl.ds(cb, 1), :]
+        rate = wide((-TAU_SCALE) / mu)
         back = (0.5 * (0.5 * SSA_MAX)) * (1.0 - ASYM * mu)
         fall = wide(0.5 * SSA_MAX - back)
         back = wide(back)
         zero = jnp.zeros((gpoints, CB), jnp.float32)
         carry = (solar * mu, zero, zero)
-        lit = litf_ref[pl.ds(cb, 1), :]
-        if ascend:
-            albedo = [albedo_ref[s, pl.ds(cb, 1), :] for s in range(2)]
-        following = None
-        if ahead:
-            following = Prepare(rate_of(order(i + 1)))
-            later = not isinstance(i, int) or i + 2 < ncb
-            if later:
-                for pair in range(2):
-                    stage_pair(order(jnp.minimum(i + 2, ncb - 1)), pair)
-                for pair in range(2):
-                    product(inputs_ref.at[pair], big_ref, next_ref.at[pair])
-        share = 0.78 if ascend else 1.0
+        after = order(jnp.minimum(i + 1, ncb - 1))
+        for pair in range(2):
+            stage_pair(after, pair)
+        for pair in range(2):
+            product(inputs_ref.at[pair], big_ref, next_ref.at[pair])
         for level in range(lev):
-            if pending is not None:
-                pending.level(lev - 1 - level)
-            carry = recur(coef_ref, level, state_ref, level, back, fall, carry)
-            if following is not None:
-                following.until(share * (level + 1))
-        if not ascend:
-            mix_ref[...] = next_ref[...]
-            return carry
-        up = Ascent(albedo, lit, carry, state_ref, rise_ref.at[0])
-        for level in range(lev):
-            up.level(lev - 1 - level)
-            if following is not None:
-                following.until(lev * (share + (1.0 - share) * (level + 1) / lev) + 1e-6)
-        if following is not None and later:
-            mix_ref[...] = next_ref[...]
-        flux_ref[cb + 1] = rise_ref[0]
-
+            chunk, j = level // CHUNK, level % CHUNK
+            left = chunk % 2 * CB
+            mix = mix_ref[chunk // 2, j * rows : (j + 1) * rows, left : left + CB]
+            carry = layer(mix, rate, back, fall, carry, state_ref, level)
+        for j in range(3):
+            end_ref[slot, j] = carry[j]
+
+    def up(i):
+        cb = order(i)
+        slot = lax.rem(i, slots)
+        albedo = [albedo_ref[s, pl.ds(cb, 1), :] for s in range(2)]
+        rise = Ascent(
+            albedo, litf_ref[pl.ds(cb, 1), :], [end_ref[slot, j] for j in range(3)],
+            states_ref.at[slot], flux_ref.at[cb + 1],
+        )
+        for level in reversed(range(lev)):
+            rise.level(level)
+
+    load.wait()
+    for pair in range(2):
+        stage_pair(0, pair)
+        product(inputs_ref.at[pair], big_ref, mix_ref.at[pair])
     pl.semaphore_wait(barrier, n - 1)
     sends = []
     for i, peer in enumerate(peers):
@@ -307,32 +280,8 @@
         copy.start()
         sends.append(copy)
 
-    load.wait()
-    multiply(0, mix_ref)
-    Prepare(rate_of(0)).until(lev)
-    multiply(order(1), mix_ref)
-    carry = step(0, True, first_ref, ascend=False)
-    for i in range(3):
-        end_ref[i] = carry[i]
-
-    for copy in sends:
-        copy.wait()
-    start_span = me * (ncb * CB // span)
-    pieces = [mine_ref[...]] + [pieces_ref[i] for i in range(n - 1)]
-    direct, diffuse = pick_albedo(pieces, start_span, span, blocks, ncb)
-    albedo_ref[0] = direct
-    albedo_ref[1] = diffuse
-    pending = Ascent(
-        [albedo_ref[s, 0:1, :] for s in range(2)], litf_ref[0:1, :], [end_ref[i] for i in range(3)],
-        first_ref, rise_ref.at[1],
-    )
-    step(1, True, state_ref, pending=pending)
-    flux_ref[1] = rise_ref[1]
-    edge_ref[0] = rise_ref[1]
-    edge_ref[1] = rise_ref[0]
-    sends = []
-    for i, peer in ((0, peers[-1]), (1, peers[0])):
-        copy = pltpu.make_async_remote_copy(
+    edges = [
+        pltpu.make_async_remote_copy(
             src_ref=edge_ref.at[i],
             dst_ref=halo_ref.at[i],
             send_sem=edge_send.at[i],
@@ -340,16 +289,52 @@
             device_id={"blk": peer},
             device_id_type=mesh_id,
         )
-        copy.start()
-        sends.append(copy)
-
-    def middle_steps(i, unused):
-        step(i, True, state_ref)
+        for i, peer in ((0, peers[-1]), (1, peers[0]))
+    ]
+
+    def early_up(i, unused):
+        up(i)
+
+        @pl.when(i == 1)
+        def _():
+            edge_ref[0] = flux_ref[1]
+            edge_ref[1] = flux_ref[ncb]
+            for copy in edges:
+                copy.start()
+
         return unused
 
-    lax.fori_loop(2, ncb - 1, middle_steps, 0)
-    step(ncb - 1, False, state_ref)
-    for copy in sends:
+    def receive():
+        for copy in sends:
+            copy.wait()
+        start_span = me * (ncb * CB // span)
+        pieces = [mine_ref[...]] + [pieces_ref[i] for i in range(n - 1)]
+        direct, diffuse = pick_albedo(pieces, start_span, span, blocks, ncb)
+        albedo_ref[0] = direct
+        albedo_ref[1] = diffuse
+        lax.fori_loop(0, slots, early_up, 0)
+
+    def two_steps(j, unused):
+        down(2 * j, mix_ref, next_ref)
+
+        @pl.when(j == 1)
+        def _():
+            receive()
+
+        @pl.when(j > 1)
+        def _():
+            up(2 * j)
+
+        down(2 * j + 1, next_ref, mix_ref)
+
+        @pl.when(j > 0)
+        def _():
+            up(2 * j + 1)
+
+        return unused
+
+    lax.fori_loop(0, ncb // 2, two_steps, 0)
+    for copy in edges:
         copy.wait()
     flux_ref[0] = halo_ref[1]
     flux_ref[ncb + 1] = halo_ref[0]
@@ -397,7 +382,7 @@
     span = cols // blocks
     rows = round_up(2 * (lev + 1), 8)
     full = pl.BlockSpec(memory_space=VMEM)
-    state = VMEM((4, lev, gpoints, CB), jnp.float32)
+    slots = 3
     fluxes = pl.pallas_call(
         functools.partial(flux_kernel, n, span),
         out_shape=jax.ShapeDtypeStruct((ncb + 2, rows, CB), jnp.float32),
@@ -405,9 +390,8 @@
         out_specs=full,
         scratch_shapes=[
             VMEM((CHUNK * 2 * gpoints, 2 * CHUNK * feats), jnp.bfloat16),
-            state,
-            state,
-            VMEM((3, gpoints, CB), jnp.float32),
+            VMEM((slots, 4, lev, gpoints, CB), jnp.float32),
+            VMEM((slots, 3, gpoints, CB), jnp.float32),
             VMEM((2, ncb, CB), jnp.float32),
             VMEM((ncb, CB), jnp.float32),
             VMEM((ncb, CB), jnp.float32),
@@ -418,8 +402,6 @@
             VMEM((2, CHUNK * feats, 2 * CB), gas_state.dtype),
             VMEM((2, CHUNK * 2 * gpoints, 2 * CB), jnp.float32),
             VMEM((2, CHUNK * 2 * gpoints, 2 * CB), jnp.float32),
-            VMEM((6, lev, gpoints, CB), jnp.float32),
-            VMEM((2, rows, CB), jnp.float32),
             VMEM((feats, lev, cols), gas_state.dtype),
             pltpu.SemaphoreType.DMA((n - 1,)),
             pltpu.SemaphoreType.DMA((n - 1,)),

time: 16.6 us -> 15.4 us (0.928)
  Pallas kernels: 16.3 us -> 15.2 us
    pallas_call x1, Pallas kernels: 14.8 us -> 13.6 us  [local(): pl.pallas_call(functools.partial(flux_kernel, n, span), out_shape=jax.Sha...]
where the time goes in v3:
time: 15.4 us; the launch traced here: 15.2 us
  Pallas kernels  15.2 us (99%)
    pallas_call x1, Pallas kernels, local(): pl.pallas_call(functools.partial(flux_kernel, n, span), out_shape=jax.Sha...  13.6 us
    pallas_call x1, Pallas kernels, local(): pl.pallas_call(side_kernel, out_shape=jax.ShapeDtypeStruct((lev + 1, 2, c...  1.55 us

profile of v3, /device:TPU:0, one launch (start us, length us, event | category | flops | bytes accessed | tf_op | source)
XLA Modules:
  0.0 15.2 jit_solution(3230380005442373494)
XLA Ops:
  0.0 0.0 copy-start
  0.0 0.0 copy-start.1
  0.0 13.6 %shard_map.100.flux_ref = f32[10,72,128]{2,1,0:T(8,128)S(1)} custom-call(bf16[16,32,1024]{2,1,0:T(8,128)(2,1)} %gas_hbm.1, bf16[8,128]{1,0:T(8,128)(2,1)} %bitcast.11, s32[8,128]{1,0:T(8,128)} %bitcast.9, bf16[16,64]{1,0:T(8,128)(2,1)} %bitcast.10, f32[1,32]{1,0:T(1,128)} %bitcast.12, f32[32,128]{1,0:T(8,128)} %bitcast.7, f32[2,4096]{1,0:T(2,128)} %fine_albedo_ref.1, ...), custom_call_target="tpu_custom_call" | custom-call | tf_op jit(solution)/shard_map/pallas_call | solution.py:386
  13.6 0.0 copy-done
  13.6 0.0 copy-done.1
  13.6 1.6 %shard_map.101 = f32[33,2,1024]{2,1,0:T(2,128)} custom-call(f32[10,72,128]{2,1,0:T(8,128)S(1)} %shard_map.100.flux_ref, s32[3,1024]{1,0:T(4,128)S(1)} %copy-done, f32[3,1024]{1,0:T(4,128)S(1)} %copy-done.1), custom_call_target="tpu_custom_call" | custom-call | tf_op jit(solution)/shard_map/pallas_call | solution.py:423
Async XLA Ops:
  0.0 13.6 %copy-start = (s32[3,1024]{1,0:T(4,128)S(1)}, s32[3,1024]{1,0:T(4,128)}, u32[]{:S(2)}) copy-start(s32[3,1024]{1,0:T(4,128)} %neighbours_ref.1) | copy-start | bytes 36868
  0.0 13.6 %copy-start.1 = (f32[3,1024]{1,0:T(4,128)S(1)}, f32[3,1024]{1,0:T(4,128)}, u32[]{:S(2)}) copy-start(f32[3,1024]{1,0:T(4,128)} %weights_ref.1) | copy-start | bytes 36868

commit v4 on v3

--- a/solution.py
+++ b/solution.py
@@ -44,24 +44,51 @@
     return first, second, number
 
 
+def own_piece(first, second, number, mine_ref):
+    span = first.shape[0]
+    per = CB // span
+    blocks = first.shape[1]
+    for i, values in enumerate((first, second)):
+        tiled = jnp.transpose(jnp.concatenate([values] * per, axis=0))
+        mine_ref[i * blocks : (i + 1) * blocks, :] = tiled.astype(jnp.bfloat16)
+    tail = mine_ref.shape[0] - 2 * blocks
+    numbers = jnp.concatenate([number] * (CB // blocks), axis=1)
+    mine_ref[2 * blocks :, :] = jnp.broadcast_to(numbers, (tail, CB)).astype(jnp.bfloat16)
+
+
 def pick_albedo(pieces, start_span, span, blocks, ncb):
     per = CB // span
-    table = jnp.concatenate(
-        [jnp.concatenate([p[0:span, s * blocks : (s + 1) * blocks] for p in pieces], axis=1) for s in range(2)],
-        axis=0,
-    ).astype(jnp.bfloat16)
-    number = jnp.concatenate([p[span : span + 1, 0:blocks] for p in pieces], axis=1).astype(jnp.int32)
-    total = number.shape[1]
-    row = lax.broadcasted_iota(jnp.int32, (ncb, total), 0) * per + start_span
-    parts = []
-    for m in range(per):
-        chosen = (number == row + m).astype(jnp.float32).astype(jnp.bfloat16)
-        parts.append(
-            lax.dot_general(chosen, table, (((1,), (1,)), ((), ())), preferred_element_type=jnp.float32)
+    group = CB // blocks
+    lane = lax.broadcasted_iota(jnp.int32, (per * ncb, CB), 1)
+    row = lax.broadcasted_iota(jnp.int32, (per * ncb, CB), 0)
+    wanted = (row % ncb * per + row // ncb + start_span).astype(jnp.float32)
+    total = None
+    for first in range(0, len(pieces), group):
+        members = pieces[first : first + group]
+        number = jnp.full((per * ncb, CB), -1.0, jnp.float32)
+        for q, piece in enumerate(members):
+            row_of = piece[2 * blocks :, :].astype(jnp.float32)[0:1]
+            number = jnp.where(lane // blocks == q, row_of, number)
+        chosen = (number == wanted).astype(jnp.float32).astype(jnp.bfloat16)
+        chosen = chosen[:, : len(members) * blocks]
+        table = jnp.concatenate(
+            [
+                jnp.concatenate([piece[i * blocks : (i + 1) * blocks, :] for piece in members], axis=0)
+                for i in range(2)
+            ],
+            axis=1,
         )
-    direct = jnp.concatenate([p[:, 0:span] for p in parts], axis=1)
-    diffuse = jnp.concatenate([p[:, span : 2 * span] for p in parts], axis=1)
-    return direct, diffuse
+        part = jnp.dot(chosen, table, preferred_element_type=jnp.float32)
+        total = part if total is None else total + part
+    lane = lax.broadcasted_iota(jnp.int32, (ncb, CB), 1)
+    results = []
+    for i in range(2):
+        result = total[0:ncb, i * CB : (i + 1) * CB]
+        for m in range(1, per):
+            part = total[m * ncb : (m + 1) * ncb, i * CB : (i + 1) * CB]
+            result = jnp.where(lane // span == m, part, result)
+        results.append(result)
+    return results
 
 
 def expand_weight(weight_ref, big_ref):
@@ -186,9 +213,10 @@
 
 
 def flux_kernel(
-    n, span, gas_hbm, cos_ref, lit_ref, weight_ref, solar_ref, area_ref, fine_albedo_ref, parent_ref,
+    n, span, gas_hbm, cos_hbm, lit_hbm, weight_hbm, solar_hbm, area_hbm, fine_albedo_hbm, parent_hbm,
     flux_ref, big_ref, states_ref, end_ref, albedo_ref, cosf_ref, litf_ref, mine_ref, pieces_ref,
-    edge_ref, halo_ref, inputs_ref, mix_ref, next_ref, gas_ref, send_sem, recv_sem, edge_send, edge_recv, gas_sem,
+    edge_ref, halo_ref, inputs_ref, mix_ref, next_ref, gas_ref, cos_ref, lit_ref, weight_ref, solar_ref,
+    area_ref, fine_albedo_ref, parent_ref, send_sem, recv_sem, edge_send, edge_recv, load_sem,
 ):
     ncb = cos_ref.shape[0]
     blocks = area_ref.shape[0]
@@ -200,21 +228,30 @@
     peers = [lax.rem(me + shift, n) for shift in range(1, n)]
     mesh_id = pl.DeviceIdType.MESH
 
-    load = pltpu.make_async_copy(gas_hbm, gas_ref, gas_sem)
-    load.start()
+    sources = [
+        (weight_hbm, weight_ref), (parent_hbm, parent_ref), (area_hbm, area_ref),
+        (fine_albedo_hbm, fine_albedo_ref), (solar_hbm, solar_ref), (cos_hbm, cos_ref), (lit_hbm, lit_ref),
+        (gas_hbm.at[:, :, 0:CB], gas_ref.at[:, :, 0:CB]), (gas_hbm.at[:, :, CB:], gas_ref.at[:, :, CB:]),
+    ]
+    loads = [pltpu.make_async_copy(src, dst, load_sem.at[i]) for i, (src, dst) in enumerate(sources)]
+    for load in loads:
+        load.start()
     barrier = pltpu.get_barrier_semaphore()
     for peer in peers:
         pl.semaphore_signal(barrier, inc=1, device_id={"blk": peer}, device_id_type=mesh_id)
 
+    for load in loads[:-1]:
+        load.wait()
+    expand_weight(weight_ref, big_ref)
+    for pair in range(2):
+        stage(0, 2 * pair * CHUNK, gas_ref, inputs_ref.at[pair])
+        product(inputs_ref.at[pair], big_ref, mix_ref.at[pair])
     first, second, number = local_albedo(area_ref, fine_albedo_ref, parent_ref, span)
-    mine_ref[...] = jnp.zeros_like(mine_ref)
-    mine_ref[0:span, 0:blocks] = first
-    mine_ref[0:span, blocks : 2 * blocks] = second
-    mine_ref[span : span + 1, 0:blocks] = number
-    expand_weight(weight_ref, big_ref)
+    own_piece(first, second, number, mine_ref)
     cosf_ref[...] = cos_ref[...].astype(jnp.float32)
     litf_ref[...] = lit_ref[...].astype(jnp.float32)
     solar = solar_column(solar_ref)
+    loads[-1].wait()
 
     def order(i):
         if isinstance(i, int):
@@ -262,14 +299,8 @@
         for level in reversed(range(lev)):
             rise.level(level)
 
-    load.wait()
-    for pair in range(2):
-        stage_pair(0, pair)
-        product(inputs_ref.at[pair], big_ref, mix_ref.at[pair])
-    pl.semaphore_wait(barrier, n - 1)
-    sends = []
-    for i, peer in enumerate(peers):
-        copy = pltpu.make_async_remote_copy(
+    sends = [
+        pltpu.make_async_remote_copy(
             src_ref=mine_ref,
             dst_ref=pieces_ref.at[i],
             send_sem=send_sem.at[i],
@@ -277,8 +308,19 @@
             device_id={"blk": peer},
             device_id_type=mesh_id,
         )
-        copy.start()
-        sends.append(copy)
+        for i, peer in enumerate(peers)
+    ]
+
+    def send():
+        pl.semaphore_wait(barrier, n - 1)
+        for copy in sends:
+            copy.start()
+
+    lower = me < n // 2
+
+    @pl.when(jnp.logical_not(lower))
+    def _():
+        send()
 
     edges = [
         pltpu.make_async_remote_copy(
@@ -308,7 +350,7 @@
         for copy in sends:
             copy.wait()
         start_span = me * (ncb * CB // span)
-        pieces = [mine_ref[...]] + [pieces_ref[i] for i in range(n - 1)]
+        pieces = [mine_ref] + [pieces_ref.at[i] for i in range(n - 1)]
         direct, diffuse = pick_albedo(pieces, start_span, span, blocks, ncb)
         albedo_ref[0] = direct
         albedo_ref[1] = diffuse
@@ -317,17 +359,21 @@
     def two_steps(j, unused):
         down(2 * j, mix_ref, next_ref)
 
+        @pl.when(j > 1)
+        def _():
+            up(2 * j)
+
+        down(2 * j + 1, next_ref, mix_ref)
+
+        @pl.when(jnp.logical_and(j == 0, lower))
+        def _():
+            send()
+
         @pl.when(j == 1)
         def _():
             receive()
 
         @pl.when(j > 1)
-        def _():
-            up(2 * j)
-
-        down(2 * j + 1, next_ref, mix_ref)
-
-        @pl.when(j > 0)
         def _():
             up(2 * j + 1)
 
@@ -382,11 +428,11 @@
     span = cols // blocks
     rows = round_up(2 * (lev + 1), 8)
     full = pl.BlockSpec(memory_space=VMEM)
-    slots = 3
+    slots = 4
     fluxes = pl.pallas_call(
         functools.partial(flux_kernel, n, span),
         out_shape=jax.ShapeDtypeStruct((ncb + 2, rows, CB), jnp.float32),
-        in_specs=[pl.BlockSpec(memory_space=pltpu.HBM)] + [full] * 7,
+        in_specs=[pl.BlockSpec(memory_space=pltpu.HBM)] * 8,
         out_specs=full,
         scratch_shapes=[
             VMEM((CHUNK * 2 * gpoints, 2 * CHUNK * feats), jnp.bfloat16),
@@ -395,19 +441,26 @@
             VMEM((2, ncb, CB), jnp.float32),
             VMEM((ncb, CB), jnp.float32),
             VMEM((ncb, CB), jnp.float32),
-            VMEM((span + 8, 128), jnp.float32),
-            VMEM((n - 1, span + 8, 128), jnp.float32),
+            VMEM((2 * blocks + 16, CB), jnp.bfloat16),
+            VMEM((n - 1, 2 * blocks + 16, CB), jnp.bfloat16),
             VMEM((2, rows, CB), jnp.float32),
             VMEM((2, rows, CB), jnp.float32),
             VMEM((2, CHUNK * feats, 2 * CB), gas_state.dtype),
             VMEM((2, CHUNK * 2 * gpoints, 2 * CB), jnp.float32),
             VMEM((2, CHUNK * 2 * gpoints, 2 * CB), jnp.float32),
             VMEM((feats, lev, cols), gas_state.dtype),
+            VMEM((ncb, CB), cos_zenith.dtype),
+            VMEM((ncb, CB), daylit.dtype),
+            VMEM((feats, 2 * gpoints), optics_weight.dtype),
+            VMEM((1, gpoints), jnp.float32),
+            VMEM((blocks, FB), jnp.float32),
+            VMEM(fine_albedo.shape, jnp.float32),
+            VMEM((blocks, FB), parent_of.dtype),
             pltpu.SemaphoreType.DMA((n - 1,)),
             pltpu.SemaphoreType.DMA((n - 1,)),
             pltpu.SemaphoreType.DMA((2,)),
             pltpu.SemaphoreType.DMA((2,)),
-            pltpu.SemaphoreType.DMA,
+            pltpu.SemaphoreType.DMA((9,)),
         ],
         compiler_params=pltpu.CompilerParams(
             collective_id=0, has_side_effects=True, vmem_limit_bytes=24 << 20

time: 15.4 us -> 13.6 us (0.88)
  Pallas kernels: 15.2 us -> 13.4 us
    pallas_call x1, Pallas kernels: 13.6 us -> 11.9 us  [local(): pl.pallas_call(functools.partial(flux_kernel, n, span), out_shape=jax.Sha...]
where the time goes in v4:
time: 13.6 us; the launch traced here: 13.5 us
  Pallas kernels  13.4 us (99%)
    pallas_call x1, Pallas kernels, local(): pl.pallas_call(functools.partial(flux_kernel, n, span), out_shape=jax.Sha...  11.9 us
    pallas_call x1, Pallas kernels, local(): pl.pallas_call(side_kernel, out_shape=jax.ShapeDtypeStruct((lev + 1, 2, c...  1.55 us

profile of v4, /device:TPU:0, one launch (start us, length us, event | category | flops | bytes accessed | tf_op | source)
XLA Modules:
  0.0 13.5 jit_solution(3357943498562355147)
XLA Ops:
  0.0 0.0 copy-start
  0.0 0.0 copy-start.1
  0.0 11.9 %shard_map.100.flux_ref = f32[10,72,128]{2,1,0:T(8,128)S(1)} custom-call(bf16[16,32,1024]{2,1,0:T(8,128)(2,1)} %gas_hbm.1, bf16[8,128]{1,0:T(8,128)(2,1)} %bitcast.11, s32[8,128]{1,0:T(8,128)} %bitcast.9, bf16[16,64]{1,0:T(8,128)(2,1)} %bitcast.10, f32[1,32]{1,0:T(1,128)} %bitcast.12, f32[32,128]{1,0:T(8,128)} %bitcast.7, f32[2,4096]{1,0:T(2,128)} %fine_albedo_hbm.1, ...), custom_call_target="tpu_custom_call" | custom-call | tf_op jit(solution)/shard_map/pallas_call | solution.py:432
  11.9 0.0 copy-done
  11.9 0.0 copy-done.1
  11.9 1.6 %shard_map.101 = f32[33,2,1024]{2,1,0:T(2,128)} custom-call(f32[10,72,128]{2,1,0:T(8,128)S(1)} %shard_map.100.flux_ref, s32[3,1024]{1,0:T(4,128)S(1)} %copy-done, f32[3,1024]{1,0:T(4,128)S(1)} %copy-done.1), custom_call_target="tpu_custom_call" | custom-call | tf_op jit(solution)/shard_map/pallas_call | solution.py:476
Async XLA Ops:
  0.0 11.9 %copy-start = (s32[3,1024]{1,0:T(4,128)S(1)}, s32[3,1024]{1,0:T(4,128)}, u32[]{:S(2)}) copy-start(s32[3,1024]{1,0:T(4,128)} %neighbours_ref.1) | copy-start | bytes 36868
  0.0 11.9 %copy-start.1 = (f32[3,1024]{1,0:T(4,128)S(1)}, f32[3,1024]{1,0:T(4,128)}, u32[]{:S(2)}) copy-start(f32[3,1024]{1,0:T(4,128)} %weights_ref.1) | copy-start | bytes 36868

commit v5 on v4

--- a/solution.py
+++ b/solution.py
@@ -278,9 +278,10 @@
         after = order(jnp.minimum(i + 1, ncb - 1))
         for pair in range(2):
             stage_pair(after, pair)
-        for pair in range(2):
-            product(inputs_ref.at[pair], big_ref, next_ref.at[pair])
         for level in range(lev):
+            for pair, place in enumerate((8, 20)):
+                if level == place:
+                    product(inputs_ref.at[pair], big_ref, next_ref.at[pair])
             chunk, j = level // CHUNK, level % CHUNK
             left = chunk % 2 * CB
             mix = mix_ref[chunk // 2, j * rows : (j + 1) * rows, left : left + CB]
@@ -354,16 +355,15 @@
         direct, diffuse = pick_albedo(pieces, start_span, span, blocks, ncb)
         albedo_ref[0] = direct
         albedo_ref[1] = diffuse
-        lax.fori_loop(0, slots, early_up, 0)
 
     def two_steps(j, unused):
         down(2 * j, mix_ref, next_ref)
 
-        @pl.when(j > 1)
-        def _():
-            up(2 * j)
-
-        down(2 * j + 1, next_ref, mix_ref)
+        def second(i, inner):
+            down(2 * j + 1, next_ref, mix_ref)
+            return inner
+
+        lax.fori_loop(0, jnp.minimum(me + 1, 1), second, 0)
 
         @pl.when(jnp.logical_and(j == 0, lower))
         def _():
@@ -373,10 +373,7 @@
         def _():
             receive()
 
-        @pl.when(j > 1)
-        def _():
-            up(2 * j + 1)
-
+        lax.fori_loop(jnp.where(j < 2, 0, 2 * j), jnp.where(j < 1, 0, 2 * j + 2), early_up, 0)
         return unused
 
     lax.fori_loop(0, ncb // 2, two_steps, 0)
@@ -386,34 +383,52 @@
     flux_ref[ncb + 1] = halo_ref[0]
 
 
-def side_kernel(flux_ref, neighbours_ref, weights_ref, out_ref):
+def side_kernel(flux_ref, neighbours_ref, weights_ref, out_hbm, out_ref, both_ref, out_sem):
     interfaces, parts, cols = out_ref.shape
     ncb = cols // CB
     rows = flux_ref.shape[1]
     start = (lax.axis_index("grp") * lax.axis_size("blk") + lax.axis_index("blk")) * cols
+
+    def split(block):
+        value = flux_ref[block]
+        high = value.astype(jnp.bfloat16).astype(jnp.float32)
+        both_ref[block] = jnp.concatenate([high, value - high], axis=0).astype(jnp.bfloat16)
+
+    place = lax.broadcasted_iota(jnp.int32, (3 * CB, CB), 0)
+    split(0)
+    split(1)
+    copies = []
     for cb in range(ncb):
+        split(cb + 2)
         own = slice(cb * CB, (cb + 1) * CB)
         picked = neighbours_ref[:, own] - (start + (cb - 1) * CB)
         weights = weights_ref[:, own]
-        lanes, blocks, shares = [], [], []
-        for k in range(3):
+        window = jnp.concatenate([both_ref[cb + j] for j in range(3)], axis=1)
+        chosen = (place == picked[0:1]).astype(jnp.float32).astype(jnp.bfloat16)
+        beside = jnp.dot(window, chosen, preferred_element_type=jnp.float32)
+        centre = flux_ref[cb + 1]
+        first = centre + weights[0:1] * (beside[:rows] + beside[rows:] - centre)
+        results = [first[r : r + 8] for r in range(0, rows, 8)]
+        for k in range(1, 3):
             row = jnp.broadcast_to(picked[k : k + 1], (8, CB))
-            lanes.append(row & (CB - 1))
-            blocks.append(row // CB)
-            shares.append(jnp.broadcast_to(weights[k : k + 1], (8, CB)))
-        results = [flux_ref[cb + 1, r : r + 8, :] for r in range(0, rows, 8)]
-        for k in range(3):
+            lanes, block = row & (CB - 1), row // CB
+            share = jnp.broadcast_to(weights[k : k + 1], (8, CB))
             for i, r in enumerate(range(0, rows, 8)):
                 near = [flux_ref[cb + j, r : r + 8, :] for j in range(3)]
                 before, here, after = [
-                    jnp.take_along_axis(v, lanes[k], axis=1, mode="promise_in_bounds") for v in near
+                    jnp.take_along_axis(v, lanes, axis=1, mode="promise_in_bounds") for v in near
                 ]
-                beside = jnp.where(blocks[k] == 0, before, jnp.where(blocks[k] == 1, here, after))
-                results[i] = results[i] + shares[k] * (beside - near[1])
+                beside = jnp.where(block == 0, before, jnp.where(block == 1, here, after))
+                results[i] = results[i] + share * (beside - near[1])
         for r, result in zip(range(0, rows, 8), results):
             top = r // parts
             count = min(8 // parts, interfaces - top)
             out_ref[top : top + count, :, own] = result[: count * parts].reshape(count, parts, CB)
+        copy = pltpu.make_async_copy(out_ref.at[:, :, own], out_hbm.at[:, :, own], out_sem.at[cb])
+        copy.start()
+        copies.append(copy)
+    for copy in copies:
+        copy.wait()
 
 
 def local(
@@ -477,7 +492,12 @@
         side_kernel,
         out_shape=jax.ShapeDtypeStruct((lev + 1, 2, cols), jnp.float32),
         in_specs=[full] * 3,
-        out_specs=full,
+        out_specs=pl.BlockSpec(memory_space=pl.ANY),
+        scratch_shapes=[
+            VMEM((lev + 1, 2, cols), jnp.float32),
+            VMEM((ncb + 2, 2 * rows, CB), jnp.bfloat16),
+            pltpu.SemaphoreType.DMA((ncb,)),
+        ],
         compiler_params=pltpu.CompilerParams(vmem_limit_bytes=8 << 20),
     )(fluxes, neighbours, side_weight)
     return jnp.transpose(result, (1, 0, 2))

time: 13.6 us -> 13.3 us (0.978)
  Pallas kernels: 13.4 us -> 13.2 us
    pallas_call x1, Pallas kernels: 1.55 us -> 1.38 us  [local(): pl.pallas_call(side_kernel, out_shape=jax.ShapeDtypeStruct((lev + 1, 2, c...]
where the time goes in v5:
time: 13.3 us; the launch traced here: 13.2 us
  Pallas kernels  13.2 us (99%)
    pallas_call x1, Pallas kernels, local(): pl.pallas_call(functools.partial(flux_kernel, n, span), out_shape=jax.Sha...  11.8 us
    pallas_call x1, Pallas kernels, local(): pl.pallas_call(side_kernel, out_shape=jax.ShapeDtypeStruct((lev + 1, 2, c...  1.38 us

profile of v5, /device:TPU:0, one launch (start us, length us, event | category | flops | bytes accessed | tf_op | source)
XLA Modules:
  0.0 13.2 jit_solution(11595974256864411758)
XLA Ops:
  0.0 0.0 copy-start
  0.0 0.0 copy-start.1
  0.0 11.8 %shard_map.100.flux_ref = f32[10,72,128]{2,1,0:T(8,128)S(1)} custom-call(bf16[16,32,1024]{2,1,0:T(8,128)(2,1)} %gas_hbm.1, bf16[8,128]{1,0:T(8,128)(2,1)} %bitcast.11, s32[8,128]{1,0:T(8,128)} %bitcast.9, bf16[16,64]{1,0:T(8,128)(2,1)} %bitcast.10, f32[1,32]{1,0:T(1,128)} %bitcast.12, f32[32,128]{1,0:T(8,128)} %bitcast.7, f32[2,4096]{1,0:T(2,128)} %fine_albedo_hbm.1, ...), custom_call_target="tpu_custom_call" | custom-call | tf_op jit(solution)/shard_map/pallas_call | solution.py:447
  11.8 0.0 copy-done
  11.8 0.0 copy-done.1
  11.8 1.4 %shard_map.101 = f32[33,2,1024]{2,1,0:T(2,128)} custom-call(f32[10,72,128]{2,1,0:T(8,128)S(1)} %shard_map.100.flux_ref, s32[3,1024]{1,0:T(4,128)S(1)} %copy-done, f32[3,1024]{1,0:T(4,128)S(1)} %copy-done.1), custom_call_target="tpu_custom_call" | custom-call | tf_op jit(solution)/shard_map/pallas_call | solution.py:491
Async XLA Ops:
  0.0 11.8 %copy-start = (s32[3,1024]{1,0:T(4,128)S(1)}, s32[3,1024]{1,0:T(4,128)}, u32[]{:S(2)}) copy-start(s32[3,1024]{1,0:T(4,128)} %neighbours_ref.1) | copy-start | bytes 36868
  0.0 11.8 %copy-start.1 = (f32[3,1024]{1,0:T(4,128)S(1)}, f32[3,1024]{1,0:T(4,128)}, u32[]{:S(2)}) copy-start(f32[3,1024]{1,0:T(4,128)} %weights_ref.1) | copy-start | bytes 36868
